TPU v7x, 128 devices: a whole 4x4x4 slice. The times are simulated.
128 devices in a mesh: gx: 128 (over z, y, x, core).
Axes of the slice: x: 4, y: 4, z: 4, core: 2. Of those that a mesh axis runs over, the one named last changes fastest.
Arguments:
- value: float32 [256, 48, 32, 128], P('gx'), may hold values from -6 to 6
- target: float32 [256, 48, 32, 128], P('gx'), may hold values from -6 to 6
- obstacle: float32 [256, 48, 32, 128], P('gx'), may hold values from -6 to -0.5
- fractions: float32 [16, 4], replicated, may hold values from 0 to 1
- control_cost: float32 [16], replicated, may hold values from 0 to 0.5
- shard_offset: int32 [16], replicated, may hold values from -8 to 8, as said below
- cell_offset: int32 [16], replicated, may hold values from 0 to 1
- grid_offset: int32 [16, 3], replicated, may hold values from -4 to 4
Outputs:
- updated: float32 [256, 48, 32, 128], P('gx')
Inputs may be any that keep to these rules, and one draw needn't show every extreme that they name: `shard_offset`: every draw holds both -8 and 8.
All inputs are finite; a program needn't handle non-finite values.
Results may differ from a plain program's by a relative error of at most 0.00002.
Values sent between devices are 32-bit elements; how exact they have to be, the bound alone decides.
A program may use at most 128 MiB of HBM per device.

v0:
```python
import jax
import jax.numpy as jnp
from jax import lax
from jax.sharding import PartitionSpec as P

NCTRL = 16
REACH = 8


def passed_along(x, axis, by):
    size = lax.axis_size(axis)
    return lax.ppermute(x, axis, [(i, (i + by) % size) for i in range(size)])


def blend(low, high, frac):
    return (1.0 - frac) * low + frac * high


def body(value, target, obstacle, fractions, control_cost, shard_offset, cell_offset, grid_offset):
    rows = value.shape[0]
    count = 2 * REACH + 2
    above = []
    current = value
    for step in range(REACH + 1):
        current = passed_along(current, "gx", -1)
        above.append(current)
    below = []
    current = value
    for step in range(REACH):
        current = passed_along(current, "gx", 1)
        below.append(current)
    pieces = below[::-1] + [value] + above

    def make_branch(offset):

        def branch(start):
            joined = jnp.concatenate([pieces[offset], pieces[offset + 1]], axis=0)
            return lax.dynamic_slice_in_dim(joined, start, rows + 1, 0)

        return branch

    branches = [make_branch(offset) for offset in range(count - 1)]

    def one_control(u, best):
        needed = lax.switch(shard_offset[u] + REACH, branches, cell_offset[u])
        field = blend(needed[:rows], needed[1:], fractions[u, 0])
        for axis_k in range(1, 4):
            moved = grid_offset[u, axis_k - 1]
            field = blend(
                jnp.roll(field, -moved, axis=axis_k),
                jnp.roll(field, -moved - 1, axis=axis_k),
                fractions[u, axis_k],
            )
        return jnp.minimum(best, field + control_cost[u])

    start = jnp.full(value.shape, jnp.inf, jnp.float32)
    best = lax.fori_loop(0, NCTRL, one_control, start)
    return jnp.maximum(obstacle, jnp.minimum(target, best))


def solution(mesh):
    return jax.shard_map(
        body,
        mesh=mesh,
        in_specs=(
            P("gx", None, None, None),
            P("gx", None, None, None),
            P("gx", None, None, None),
            P(),
            P(),
            P(),
            P(),
            P(),
        ),
        out_specs=P("gx", None, None, None),
        check_vma=False,
    )
```

profile of v0, /device:TPU:0, one launch (start us, length us, event | category | flops | bytes accessed | tf_op | source)
XLA Modules:
  0.0 655.4 jit_solution(16560613202821557267)
XLA Ops:
  0.0 8.2 %collective-permute-start.8 = (f32[2,48,32,128]{3,2,1,0:T(8,128)}, f32[2,48,32,128]{3,2,1,0:T(8,128)S(1)}, u32[]{:S(2)}, u32[]{:S(2)}) collective-permute-start(f32[2,48,32,128]{3,2,1,0:T(8,128)} %param.33), channel_id=1, source_target_pairs={{0,127},{1,0},{2,1},{3,2},{4,3},{5,4},{6,5},{7,6},{8,7},{9,8},{10,... | collective-permute-start | bytes 4718600 | tf_op jit(solution)/shard_map/ppermute | solution.py:12
  8.2 18.2 %collective-permute-done.8 = f32[2,48,32,128]{3,2,1,0:T(8,128)S(1)} collective-permute-done((f32[2,48,32,128]{3,2,1,0:T(8,128)}, f32[2,48,32,128]{3,2,1,0:T(8,128)S(1)}, u32[]{:S(2)}, u32[]{:S(2)}) %collective-permute-start.8) | collective-permute-done | bytes 1572896 | tf_op jit(solution)/shard_map/ppermute | solution.py:12
  27.6 7.2 %collective-permute-start.9 = (f32[2,48,32,128]{3,2,1,0:T(8,128)S(1)}, f32[2,48,32,128]{3,2,1,0:T(8,128)S(1)}, u32[]{:S(2)}, u32[]{:S(2)}) collective-permute-start(f32[2,48,32,128]{3,2,1,0:T(8,128)S(1)} %collective-permute-done.8), channel_id=1, source_target_pairs={{0,127},{1,0},{2,1},{3,2},{4,3},{5,4},{6,5},{7,6},{8,7},{9,8},{10,... | collective-permute-start | bytes 4718600 | tf_op jit(solution)/shard_map/ppermute | solution.py:12
  34.9 17.9 %collective-permute-done.9 = f32[2,48,32,128]{3,2,1,0:T(8,128)S(1)} collective-permute-done((f32[2,48,32,128]{3,2,1,0:T(8,128)S(1)}, f32[2,48,32,128]{3,2,1,0:T(8,128)S(1)}, u32[]{:S(2)}, u32[]{:S(2)}) %collective-permute-start.9) | collective-permute-done | bytes 1572896 | tf_op jit(solution)/shard_map/ppermute | solution.py:12
  52.8 7.3 %collective-permute-start.10 = (f32[2,48,32,128]{3,2,1,0:T(8,128)S(1)}, f32[2,48,32,128]{3,2,1,0:T(8,128)S(1)}, u32[]{:S(2)}, u32[]{:S(2)}) collective-permute-start(f32[2,48,32,128]{3,2,1,0:T(8,128)S(1)} %collective-permute-done.9), channel_id=1, source_target_pairs={{0,127},{1,0},{2,1},{3,2},{4,3},{5,4},{6,5},{7,6},{8,7},{9,8},{10,... | collective-permute-start | bytes 4718600 | tf_op jit(solution)/shard_map/ppermute | solution.py:12
  60.2 17.8 %collective-permute-done.10 = f32[2,48,32,128]{3,2,1,0:T(8,128)S(1)} collective-permute-done((f32[2,48,32,128]{3,2,1,0:T(8,128)S(1)}, f32[2,48,32,128]{3,2,1,0:T(8,128)S(1)}, u32[]{:S(2)}, u32[]{:S(2)}) %collective-permute-start.10) | collective-permute-done | bytes 1572896 | tf_op jit(solution)/shard_map/ppermute | solution.py:12
  78.1 7.3 %collective-permute-start.11 = (f32[2,48,32,128]{3,2,1,0:T(8,128)S(1)}, f32[2,48,32,128]{3,2,1,0:T(8,128)S(1)}, u32[]{:S(2)}, u32[]{:S(2)}) collective-permute-start(f32[2,48,32,128]{3,2,1,0:T(8,128)S(1)} %collective-permute-done.10), channel_id=1, source_target_pairs={{0,127},{1,0},{2,1},{3,2},{4,3},{5,4},{6,5},{7,6},{8,7},{9,8},{10,... | collective-permute-start | bytes 4718600 | tf_op jit(solution)/shard_map/ppermute | solution.py:12
  85.5 17.8 %collective-permute-done.11 = f32[2,48,32,128]{3,2,1,0:T(8,128)S(1)} collective-permute-done((f32[2,48,32,128]{3,2,1,0:T(8,128)S(1)}, f32[2,48,32,128]{3,2,1,0:T(8,128)S(1)}, u32[]{:S(2)}, u32[]{:S(2)}) %collective-permute-start.11) | collective-permute-done | bytes 1572896 | tf_op jit(solution)/shard_map/ppermute | solution.py:12
  103.4 7.3 %collective-permute-start.12 = (f32[2,48,32,128]{3,2,1,0:T(8,128)S(1)}, f32[2,48,32,128]{3,2,1,0:T(8,128)S(1)}, u32[]{:S(2)}, u32[]{:S(2)}) collective-permute-start(f32[2,48,32,128]{3,2,1,0:T(8,128)S(1)} %collective-permute-done.11), channel_id=1, source_target_pairs={{0,127},{1,0},{2,1},{3,2},{4,3},{5,4},{6,5},{7,6},{8,7},{9,8},{10,... | collective-permute-start | bytes 4718600 | tf_op jit(solution)/shard_map/ppermute | solution.py:12
  110.8 17.8 %collective-permute-done.12 = f32[2,48,32,128]{3,2,1,0:T(8,128)S(1)} collective-permute-done((f32[2,48,32,128]{3,2,1,0:T(8,128)S(1)}, f32[2,48,32,128]{3,2,1,0:T(8,128)S(1)}, u32[]{:S(2)}, u32[]{:S(2)}) %collective-permute-start.12) | collective-permute-done | bytes 1572896 | tf_op jit(solution)/shard_map/ppermute | solution.py:12
  128.6 7.3 %collective-permute-start.13 = (f32[2,48,32,128]{3,2,1,0:T(8,128)S(1)}, f32[2,48,32,128]{3,2,1,0:T(8,128)S(1)}, u32[]{:S(2)}, u32[]{:S(2)}) collective-permute-start(f32[2,48,32,128]{3,2,1,0:T(8,128)S(1)} %collective-permute-done.12), channel_id=1, source_target_pairs={{0,127},{1,0},{2,1},{3,2},{4,3},{5,4},{6,5},{7,6},{8,7},{9,8},{10,... | collective-permute-start | bytes 4718600 | tf_op jit(solution)/shard_map/ppermute | solution.py:12
  136.1 17.8 %collective-permute-done.13 = f32[2,48,32,128]{3,2,1,0:T(8,128)S(1)} collective-permute-done((f32[2,48,32,128]{3,2,1,0:T(8,128)S(1)}, f32[2,48,32,128]{3,2,1,0:T(8,128)S(1)}, u32[]{:S(2)}, u32[]{:S(2)}) %collective-permute-start.13) | collective-permute-done | bytes 1572896 | tf_op jit(solution)/shard_map/ppermute | solution.py:12
  153.9 7.3 %collective-permute-start.14 = (f32[2,48,32,128]{3,2,1,0:T(8,128)S(1)}, f32[2,48,32,128]{3,2,1,0:T(8,128)S(1)}, u32[]{:S(2)}, u32[]{:S(2)}) collective-permute-start(f32[2,48,32,128]{3,2,1,0:T(8,128)S(1)} %collective-permute-done.13), channel_id=1, source_target_pairs={{0,127},{1,0},{2,1},{3,2},{4,3},{5,4},{6,5},{7,6},{8,7},{9,8},{10,... | collective-permute-start | bytes 4718600 | tf_op jit(solution)/shard_map/ppermute | solution.py:12
  161.3 17.8 %collective-permute-done.14 = f32[2,48,32,128]{3,2,1,0:T(8,128)S(1)} collective-permute-done((f32[2,48,32,128]{3,2,1,0:T(8,128)S(1)}, f32[2,48,32,128]{3,2,1,0:T(8,128)S(1)}, u32[]{:S(2)}, u32[]{:S(2)}) %collective-permute-start.14) | collective-permute-done | bytes 1572896 | tf_op jit(solution)/shard_map/ppermute | solution.py:12
  179.2 7.3 %collective-permute-start.15 = (f32[2,48,32,128]{3,2,1,0:T(8,128)S(1)}, f32[2,48,32,128]{3,2,1,0:T(8,128)S(1)}, u32[]{:S(2)}, u32[]{:S(2)}) collective-permute-start(f32[2,48,32,128]{3,2,1,0:T(8,128)S(1)} %collective-permute-done.14), channel_id=1, source_target_pairs={{0,127},{1,0},{2,1},{3,2},{4,3},{5,4},{6,5},{7,6},{8,7},{9,8},{10,... | collective-permute-start | bytes 4718600 | tf_op jit(solution)/shard_map/ppermute | solution.py:12
  186.7 17.8 %collective-permute-done.15 = f32[2,48,32,128]{3,2,1,0:T(8,128)S(1)} collective-permute-done((f32[2,48,32,128]{3,2,1,0:T(8,128)S(1)}, f32[2,48,32,128]{3,2,1,0:T(8,128)S(1)}, u32[]{:S(2)}, u32[]{:S(2)}) %collective-permute-start.15) | collective-permute-done | bytes 1572896 | tf_op jit(solution)/shard_map/ppermute | solution.py:12
  204.5 7.3 %collective-permute-start.16 = (f32[2,48,32,128]{3,2,1,0:T(8,128)S(1)}, f32[2,48,32,128]{3,2,1,0:T(8,128)}, u32[]{:S(2)}, u32[]{:S(2)}) collective-permute-start(f32[2,48,32,128]{3,2,1,0:T(8,128)S(1)} %collective-permute-done.15), channel_id=1, source_target_pairs={{0,127},{1,0},{2,1},{3,2},{4,3},{5,4},{6,5},{7,6},{8,7},{9,8},{10,... | collective-permute-start | bytes 4718600 | tf_op jit(solution)/shard_map/ppermute | solution.py:12
  212.3 17.4 %collective-permute-done.16 = f32[2,48,32,128]{3,2,1,0:T(8,128)} collective-permute-done((f32[2,48,32,128]{3,2,1,0:T(8,128)S(1)}, f32[2,48,32,128]{3,2,1,0:T(8,128)}, u32[]{:S(2)}, u32[]{:S(2)}) %collective-permute-start.16) | collective-permute-done | bytes 1572896 | tf_op jit(solution)/shard_map/ppermute | solution.py:12
  229.7 421.6 %while.17 = (s32[]{:T(128)}, f32[2,48,32,128]{3,2,1,0:T(8,128)}, f32[16,4]{0,1:T(4,128)}, s32[16]{0:T(128)}, s32[16]{0:T(128)}, /*index=5*/f32[2,48,32,128]{3,2,...) while((s32[]{:T(128)}, f32[2,48,32,128]{3,2,1,0:T(8,128)}, ...), condition=%wide.region_18.22_spmd.clone, body=%wide.region_0.21_spmd.clone.sunk | while | flops 9044067 | bytes 40898644 | solution.py:57
  250.3 4.2 fusion.25
  266.9 3.3 fusion.23
  275.1 5.6 fusion.25
  301.3 5.6 fusion.25
  319.3 3.4 fusion.23
  327.6 5.6 fusion.25
  336.3 3.4 conditional.3
  346.7 3.3 fusion.23
  354.9 5.6 fusion.25
  381.1 5.6 fusion.25
  399.1 3.4 fusion.23
  407.4 5.6 fusion.25
  433.6 5.6 fusion.25
  451.6 3.4 fusion.23
  459.8 5.6 fusion.25
  477.8 3.4 fusion.23
  486.1 5.6 fusion.25
  504.1 3.3 fusion.23
  512.4 5.6 fusion.25
  521.1 3.4 conditional.3
  531.5 3.4 fusion.23
  539.8 5.6 fusion.25
  566.0 5.6 fusion.25
  592.2 5.6 fusion.25
  618.3 5.6 fusion.25
  627.0 3.4 conditional.3
  637.5 3.4 fusion.23
  645.8 5.6 fusion.25
  651.4 4.0 minimum_maximum_fusion
  (357 shorter events, 225.0 us)
Async XLA Ops:
  0.0 26.5 %collective-permute-start.8 = (f32[2,48,32,128]{3,2,1,0:T(8,128)}, f32[2,48,32,128]{3,2,1,0:T(8,128)S(1)}, u32[]{:S(2)}, u32[]{:S(2)}) collective-permute-start(f32[2,48,32,128]{3,2,1,0:T(8,128)} %param.33), channel_id=1, source_target_pairs={{0,127},{1,0},{2,1},{3,2},{4,3},{5,4},{6,5},{7,6},{8,7},{9,8},{10,... | collective-permute-start | bytes 4718600 | tf_op jit(solution)/shard_map/ppermute | solution.py:12
  8.2 26.6 %collective-permute-start = (f32[2,48,32,128]{3,2,1,0:T(8,128)}, f32[2,48,32,128]{3,2,1,0:T(8,128)S(1)}, u32[]{:S(2)}, u32[]{:S(2)}) collective-permute-start(f32[2,48,32,128]{3,2,1,0:T(8,128)} %param.33), channel_id=1, source_target_pairs={{0,1},{1,2},{2,3},{3,4},{4,5},{5,6},{6,7},{7,8},{8,9},{9,10},{10,1... | collective-permute-start | bytes 4718600 | tf_op jit(solution)/shard_map/ppermute | solution.py:12
  27.6 25.2 %collective-permute-start.9 = (f32[2,48,32,128]{3,2,1,0:T(8,128)S(1)}, f32[2,48,32,128]{3,2,1,0:T(8,128)S(1)}, u32[]{:S(2)}, u32[]{:S(2)}) collective-permute-start(f32[2,48,32,128]{3,2,1,0:T(8,128)S(1)} %collective-permute-done.8), channel_id=1, source_target_pairs={{0,127},{1,0},{2,1},{3,2},{4,3},{5,4},{6,5},{7,6},{8,7},{9,8},{10,... | collective-permute-start | bytes 4718600 | tf_op jit(solution)/shard_map/ppermute | solution.py:12
  34.9 17.9 %copy-start.1 = (f32[2,48,32,128]{3,2,1,0:T(8,128)}, f32[2,48,32,128]{3,2,1,0:T(8,128)S(1)}, u32[]{:S(2)}) copy-start(f32[2,48,32,128]{3,2,1,0:T(8,128)S(1)} %collective-permute-done) | copy-start | bytes 4718596
  34.9 25.3 %collective-permute-start.1 = (f32[2,48,32,128]{3,2,1,0:T(8,128)S(1)}, f32[2,48,32,128]{3,2,1,0:T(8,128)S(1)}, u32[]{:S(2)}, u32[]{:S(2)}) collective-permute-start(f32[2,48,32,128]{3,2,1,0:T(8,128)S(1)} %collective-permute-done), channel_id=1, source_target_pairs={{0,1},{1,2},{2,3},{3,4},{4,5},{5,6},{6,7},{7,8},{8,9},{9,10},{10,1... | collective-permute-start | bytes 4718600 | tf_op jit(solution)/shard_map/ppermute | solution.py:12
  52.8 7.3 %copy-start.2 = (f32[2,48,32,128]{3,2,1,0:T(8,128)}, f32[2,48,32,128]{3,2,1,0:T(8,128)S(1)}, u32[]{:S(2)}) copy-start(f32[2,48,32,128]{3,2,1,0:T(8,128)S(1)} %collective-permute-done.9) | copy-start | bytes 4718596
  52.8 25.3 %collective-permute-start.10 = (f32[2,48,32,128]{3,2,1,0:T(8,128)S(1)}, f32[2,48,32,128]{3,2,1,0:T(8,128)S(1)}, u32[]{:S(2)}, u32[]{:S(2)}) collective-permute-start(f32[2,48,32,128]{3,2,1,0:T(8,128)S(1)} %collective-permute-done.9), channel_id=1, source_target_pairs={{0,127},{1,0},{2,1},{3,2},{4,3},{5,4},{6,5},{7,6},{8,7},{9,8},{10,... | collective-permute-start | bytes 4718600 | tf_op jit(solution)/shard_map/ppermute | solution.py:12
  60.1 17.9 %copy-start.3 = (f32[2,48,32,128]{3,2,1,0:T(8,128)}, f32[2,48,32,128]{3,2,1,0:T(8,128)S(1)}, u32[]{:S(2)}) copy-start(f32[2,48,32,128]{3,2,1,0:T(8,128)S(1)} %collective-permute-done.1) | copy-start | bytes 4718596
  60.1 25.3 %collective-permute-start.2 = (f32[2,48,32,128]{3,2,1,0:T(8,128)S(1)}, f32[2,48,32,128]{3,2,1,0:T(8,128)S(1)}, u32[]{:S(2)}, u32[]{:S(2)}) collective-permute-start(f32[2,48,32,128]{3,2,1,0:T(8,128)S(1)} %collective-permute-done.1), channel_id=1, source_target_pairs={{0,1},{1,2},{2,3},{3,4},{4,5},{5,6},{6,7},{7,8},{8,9},{9,10},{10,1... | collective-permute-start | bytes 4718600 | tf_op jit(solution)/shard_map/ppermute | solution.py:12
  78.1 7.4 %copy-start.4 = (f32[2,48,32,128]{3,2,1,0:T(8,128)}, f32[2,48,32,128]{3,2,1,0:T(8,128)S(1)}, u32[]{:S(2)}) copy-start(f32[2,48,32,128]{3,2,1,0:T(8,128)S(1)} %collective-permute-done.10) | copy-start | bytes 4718596
  78.1 25.3 %collective-permute-start.11 = (f32[2,48,32,128]{3,2,1,0:T(8,128)S(1)}, f32[2,48,32,128]{3,2,1,0:T(8,128)S(1)}, u32[]{:S(2)}, u32[]{:S(2)}) collective-permute-start(f32[2,48,32,128]{3,2,1,0:T(8,128)S(1)} %collective-permute-done.10), channel_id=1, source_target_pairs={{0,127},{1,0},{2,1},{3,2},{4,3},{5,4},{6,5},{7,6},{8,7},{9,8},{10,... | collective-permute-start | bytes 4718600 | tf_op jit(solution)/shard_map/ppermute | solution.py:12
  85.5 17.9 %copy-start.5 = (f32[2,48,32,128]{3,2,1,0:T(8,128)}, f32[2,48,32,128]{3,2,1,0:T(8,128)S(1)}, u32[]{:S(2)}) copy-start(f32[2,48,32,128]{3,2,1,0:T(8,128)S(1)} %collective-permute-done.2) | copy-start | bytes 4718596
  85.5 25.3 %collective-permute-start.3 = (f32[2,48,32,128]{3,2,1,0:T(8,128)S(1)}, f32[2,48,32,128]{3,2,1,0:T(8,128)S(1)}, u32[]{:S(2)}, u32[]{:S(2)}) collective-permute-start(f32[2,48,32,128]{3,2,1,0:T(8,128)S(1)} %collective-permute-done.2), channel_id=1, source_target_pairs={{0,1},{1,2},{2,3},{3,4},{4,5},{5,6},{6,7},{7,8},{8,9},{9,10},{10,1... | collective-permute-start | bytes 4718600 | tf_op jit(solution)/shard_map/ppermute | solution.py:12
  103.4 7.4 %copy-start.6 = (f32[2,48,32,128]{3,2,1,0:T(8,128)}, f32[2,48,32,128]{3,2,1,0:T(8,128)S(1)}, u32[]{:S(2)}) copy-start(f32[2,48,32,128]{3,2,1,0:T(8,128)S(1)} %collective-permute-done.11) | copy-start | bytes 4718596
  103.4 25.3 %collective-permute-start.12 = (f32[2,48,32,128]{3,2,1,0:T(8,128)S(1)}, f32[2,48,32,128]{3,2,1,0:T(8,128)S(1)}, u32[]{:S(2)}, u32[]{:S(2)}) collective-permute-start(f32[2,48,32,128]{3,2,1,0:T(8,128)S(1)} %collective-permute-done.11), channel_id=1, source_target_pairs={{0,127},{1,0},{2,1},{3,2},{4,3},{5,4},{6,5},{7,6},{8,7},{9,8},{10,... | collective-permute-start | bytes 4718600 | tf_op jit(solution)/shard_map/ppermute | solution.py:12
  110.8 17.9 %copy-start.7 = (f32[2,48,32,128]{3,2,1,0:T(8,128)}, f32[2,48,32,128]{3,2,1,0:T(8,128)S(1)}, u32[]{:S(2)}) copy-start(f32[2,48,32,128]{3,2,1,0:T(8,128)S(1)} %collective-permute-done.3) | copy-start | bytes 4718596
  110.8 25.3 %collective-permute-start.4 = (f32[2,48,32,128]{3,2,1,0:T(8,128)S(1)}, f32[2,48,32,128]{3,2,1,0:T(8,128)S(1)}, u32[]{:S(2)}, u32[]{:S(2)}) collective-permute-start(f32[2,48,32,128]{3,2,1,0:T(8,128)S(1)} %collective-permute-done.3), channel_id=1, source_target_pairs={{0,1},{1,2},{2,3},{3,4},{4,5},{5,6},{6,7},{7,8},{8,9},{9,10},{10,1... | collective-permute-start | bytes 4718600 | tf_op jit(solution)/shard_map/ppermute | solution.py:12
  128.6 7.4 %copy-start.8 = (f32[2,48,32,128]{3,2,1,0:T(8,128)}, f32[2,48,32,128]{3,2,1,0:T(8,128)S(1)}, u32[]{:S(2)}) copy-start(f32[2,48,32,128]{3,2,1,0:T(8,128)S(1)} %collective-permute-done.12) | copy-start | bytes 4718596
  128.6 25.3 %collective-permute-start.13 = (f32[2,48,32,128]{3,2,1,0:T(8,128)S(1)}, f32[2,48,32,128]{3,2,1,0:T(8,128)S(1)}, u32[]{:S(2)}, u32[]{:S(2)}) collective-permute-start(f32[2,48,32,128]{3,2,1,0:T(8,128)S(1)} %collective-permute-done.12), channel_id=1, source_target_pairs={{0,127},{1,0},{2,1},{3,2},{4,3},{5,4},{6,5},{7,6},{8,7},{9,8},{10,... | collective-permute-start | bytes 4718600 | tf_op jit(solution)/shard_map/ppermute | solution.py:12
  136.0 17.9 %copy-start.9 = (f32[2,48,32,128]{3,2,1,0:T(8,128)}, f32[2,48,32,128]{3,2,1,0:T(8,128)S(1)}, u32[]{:S(2)}) copy-start(f32[2,48,32,128]{3,2,1,0:T(8,128)S(1)} %collective-permute-done.4) | copy-start | bytes 4718596
  136.0 25.3 %collective-permute-start.5 = (f32[2,48,32,128]{3,2,1,0:T(8,128)S(1)}, f32[2,48,32,128]{3,2,1,0:T(8,128)S(1)}, u32[]{:S(2)}, u32[]{:S(2)}) collective-permute-start(f32[2,48,32,128]{3,2,1,0:T(8,128)S(1)} %collective-permute-done.4), channel_id=1, source_target_pairs={{0,1},{1,2},{2,3},{3,4},{4,5},{5,6},{6,7},{7,8},{8,9},{9,10},{10,1... | collective-permute-start | bytes 4718600 | tf_op jit(solution)/shard_map/ppermute | solution.py:12
  153.9 7.4 %copy-start.10 = (f32[2,48,32,128]{3,2,1,0:T(8,128)}, f32[2,48,32,128]{3,2,1,0:T(8,128)S(1)}, u32[]{:S(2)}) copy-start(f32[2,48,32,128]{3,2,1,0:T(8,128)S(1)} %collective-permute-done.13) | copy-start | bytes 4718596
  153.9 25.3 %collective-permute-start.14 = (f32[2,48,32,128]{3,2,1,0:T(8,128)S(1)}, f32[2,48,32,128]{3,2,1,0:T(8,128)S(1)}, u32[]{:S(2)}, u32[]{:S(2)}) collective-permute-start(f32[2,48,32,128]{3,2,1,0:T(8,128)S(1)} %collective-permute-done.13), channel_id=1, source_target_pairs={{0,127},{1,0},{2,1},{3,2},{4,3},{5,4},{6,5},{7,6},{8,7},{9,8},{10,... | collective-permute-start | bytes 4718600 | tf_op jit(solution)/shard_map/ppermute | solution.py:12
  161.3 17.9 %copy-start.11 = (f32[2,48,32,128]{3,2,1,0:T(8,128)}, f32[2,48,32,128]{3,2,1,0:T(8,128)S(1)}, u32[]{:S(2)}) copy-start(f32[2,48,32,128]{3,2,1,0:T(8,128)S(1)} %collective-permute-done.5) | copy-start | bytes 4718596
  161.3 25.4 %collective-permute-start.6 = (f32[2,48,32,128]{3,2,1,0:T(8,128)S(1)}, f32[2,48,32,128]{3,2,1,0:T(8,128)}, u32[]{:S(2)}, u32[]{:S(2)}) collective-permute-start(f32[2,48,32,128]{3,2,1,0:T(8,128)S(1)} %collective-permute-done.5), channel_id=1, source_target_pairs={{0,1},{1,2},{2,3},{3,4},{4,5},{5,6},{6,7},{7,8},{8,9},{9,10},{10,1... | collective-permute-start | bytes 4718600 | tf_op jit(solution)/shard_map/ppermute | solution.py:12
  179.2 7.5 %copy-start.12 = (f32[2,48,32,128]{3,2,1,0:T(8,128)}, f32[2,48,32,128]{3,2,1,0:T(8,128)S(1)}, u32[]{:S(2)}) copy-start(f32[2,48,32,128]{3,2,1,0:T(8,128)S(1)} %collective-permute-done.14) | copy-start | bytes 4718596
  179.2 25.3 %collective-permute-start.15 = (f32[2,48,32,128]{3,2,1,0:T(8,128)S(1)}, f32[2,48,32,128]{3,2,1,0:T(8,128)S(1)}, u32[]{:S(2)}, u32[]{:S(2)}) collective-permute-start(f32[2,48,32,128]{3,2,1,0:T(8,128)S(1)} %collective-permute-done.14), channel_id=1, source_target_pairs={{0,127},{1,0},{2,1},{3,2},{4,3},{5,4},{6,5},{7,6},{8,7},{9,8},{10,... | collective-permute-start | bytes 4718600 | tf_op jit(solution)/shard_map/ppermute | solution.py:12
  186.7 25.6 %collective-permute-start.7 = (f32[2,48,32,128]{3,2,1,0:T(8,128)}, f32[2,48,32,128]{3,2,1,0:T(8,128)}, u32[]{:S(2)}, u32[]{:S(2)}) collective-permute-start(f32[2,48,32,128]{3,2,1,0:T(8,128)} %collective-permute-done.6), channel_id=1, source_target_pairs={{0,1},{1,2},{2,3},{3,4},{4,5},{5,6},{6,7},{7,8},{8,9},{9,10},{10,1... | collective-permute-start | bytes 4718600 | tf_op jit(solution)/shard_map/ppermute | solution.py:12
  204.5 25.3 %collective-permute-start.16 = (f32[2,48,32,128]{3,2,1,0:T(8,128)S(1)}, f32[2,48,32,128]{3,2,1,0:T(8,128)}, u32[]{:S(2)}, u32[]{:S(2)}) collective-permute-start(f32[2,48,32,128]{3,2,1,0:T(8,128)S(1)} %collective-permute-done.15), channel_id=1, source_target_pairs={{0,127},{1,0},{2,1},{3,2},{4,3},{5,4},{6,5},{7,6},{8,7},{9,8},{10,... | collective-permute-start | bytes 4718600 | tf_op jit(solution)/shard_map/ppermute | solution.py:12
  250.3 4.2 copy-start.14
  275.1 5.6 copy-start.14
  301.3 5.6 copy-start.14
  327.6 5.6 copy-start.14
  336.2 5.1 copy-start.17
  354.9 5.6 copy-start.14
  381.1 5.6 copy-start.14
  407.4 5.6 copy-start.14
  433.6 5.6 copy-start.14
  459.8 5.6 copy-start.14
  486.1 5.6 copy-start.14
  512.4 5.6 copy-start.14
  521.1 5.1 copy-start.17
  539.8 5.6 copy-start.14
  566.0 5.6 copy-start.14
  592.2 5.6 copy-start.14
  618.3 5.6 copy-start.14
  627.0 5.1 copy-start.17
  645.8 5.6 copy-start.14
  (65 other events, 186.5 us)
where the time goes:
time: 658 us; the launch traced here: 655 us
  other arithmetic  242 us (37%)
  waiting for transfers between devices  162 us (25%)
  loops' own time  109 us (17%)
  local copies, waits for them, and re-layouts  75.4 us (11%)
  starting transfers between devices  66.9 us (10%)
    ppermute x17, waiting for transfers between devices, passed_along(): return lax.ppermute(x, axis, [(i, (i + by) % size) for i in range(size)])  162 us
    add x48, other arithmetic, blend(): return (1.0 - frac) * low + frac * high  115 us
    another operation x1, loops' own time, body(): best = lax.fori_loop(0, NCTRL, one_control, start)  109 us
    min x16, other arithmetic, one_control(): return jnp.minimum(best, field + control_cost[u])  88.3 us
    ppermute x17, starting transfers between devices, passed_along(): return lax.ppermute(x, axis, [(i, (i + by) % size) for i in range(size)])  66.9 us
    dynamic_slice x32, local copies, waits for them, and re-layouts, one_control(): needed = lax.switch(shard_offset[u] + REACH, branches, cell_offset[u])  39.2 us
    concatenate x16, other arithmetic, branch(): joined = jnp.concatenate([pieces[offset], pieces[offset + 1]], axis=0)  35 us
  transfers between devices with their start and end apart: 17, of which 15 were waited for; matrix products, arithmetic and copies ran while one was open for 0% of the time, Pallas kernels for 0%

commit v1 on v0

v1 whole, which is shorter than its diff:
```python
import functools

import jax
import jax.numpy as jnp
from jax import lax
from jax.experimental import pallas as pl
from jax.experimental.pallas import tpu as pltpu
from jax.sharding import PartitionSpec as P

CX, NY, NZ, NW, NCTRL = 2, 48, 32, 128, 16
ROW = 8
RX = ROW * CX
LO, HI = 4, 5
ENDS = (17, 29, 41, 48)
STAGES = len(ENDS)
CUTS = (0,) + ENDS
OUTS = (0,) + tuple(e - LO - HI for e in ENDS[:-1]) + (NY,)
G, ZT = 4, 2
MESH = pl.DeviceIdType.MESH
(RIGHT, LEFT, FWD_R, FWD_L, D_OWN, D_L, D_R, D_O0, D_O1, HALO, D_HALO, HALO2, UP, DOWN) = range(14)
KINDS = 14


def kernel(frac, cost, so, co, go, value, target, obstacle, out,
           B, C, P1, Pm, Q1, Qm, A, T, O, ip, fp, ssem, rsem, lsem):
    n = lax.axis_size("gx")
    me = lax.axis_index("gx")
    j = lax.rem(me, ROW)
    base = me - j
    core = lax.rem(j, 2)
    jr, jl, jo, jp = lax.rem(j + 2, ROW), lax.rem(j + 6, ROW), lax.rem(j + 4, ROW), j + 1 - 2 * core
    qr, ql, qo = jr + 1 - 2 * core, jl + 1 - 2 * core, jo + 1 - 2 * core
    right, left, mate = base + jr, base + jl, base + jp
    up, down = lax.rem(me + ROW, n), lax.rem(me + n - ROW, n)
    last = j == ROW - 1

    loads = [pltpu.make_async_copy(value, B.at[j], lsem.at[0]),
             pltpu.make_async_copy(target, T, lsem.at[1]),
             pltpu.make_async_copy(obstacle, O, lsem.at[2])]
    loads[0].start()

    barrier = pltpu.get_barrier_semaphore()
    for peer in (right, left, mate, up, down):
        pl.semaphore_signal(barrier, inc=1, device_id=(peer,), device_id_type=MESH)

    def params(u, _):
        off = 2 * so[u] + co[u]
        for i in range(2):
            q = 2 * j + i + off
            d = jnp.where(q < 0, -1, jnp.where(q < RX, 0, 1))
            ip[i * NCTRL + u] = q - RX * d
            for e, which in enumerate((0, 1, -1)):
                fp[(8 + 3 * i + e) * NCTRL + u] = jnp.where(d == which, cost[u], jnp.inf)
        ip[2 * NCTRL + u] = go[u, 0]
        ip[3 * NCTRL + u] = go[u, 1] + 8
        ip[4 * NCTRL + u] = (NW - go[u, 2]) & (NW - 1)
        ip[5 * NCTRL + u] = (NW - 1 - go[u, 2]) & (NW - 1)
        f0, f1, f2, f3 = frac[u, 0], frac[u, 1], frac[u, 2], frac[u, 3]
        fp[u] = (1.0 - f0) * (1.0 - f2)
        fp[NCTRL + u] = (1.0 - f0) * f2
        fp[2 * NCTRL + u] = f0 * (1.0 - f2)
        fp[3 * NCTRL + u] = f0 * f2
        fp[4 * NCTRL + u] = 1.0 - f1
        fp[5 * NCTRL + u] = f1
        fp[6 * NCTRL + u] = 1.0 - f3
        fp[7 * NCTRL + u] = f3
        return 0

    lax.fori_loop(0, NCTRL, params, 0)
    loads[0].wait()
    pl.semaphore_wait(barrier, 5)

    def remote(kind, k, src, dst, peer):
        return pltpu.make_async_remote_copy(src_ref=src, dst_ref=dst, send_sem=ssem.at[kind, k],
                                            recv_sem=rsem.at[kind, k], device_id=(peer,), device_id_type=MESH)

    def block(slab, k, row=None):
        ys = pl.ds(CUTS[k], CUTS[k + 1] - CUTS[k])
        return B.at[slab, :, ys] if row is None else B.at[slab, row, ys]

    def same(kind, k, peer, slab, row=None):
        return remote(kind, k, block(slab, k, row), block(slab, k, row), peer)

    def send(kind, k):
        return {
            RIGHT: lambda: same(kind, k, right, j),
            LEFT: lambda: same(kind, k, left, j),
            FWD_R: lambda: same(kind, k, right, jl, 0),
            FWD_L: lambda: same(kind, k, left, jr, 1),
            D_OWN: lambda: same(kind, k, mate, j),
            D_L: lambda: same(kind, k, mate, jl),
            D_R: lambda: same(kind, k, mate, jr),
            D_O0: lambda: same(kind, k, mate, jo, 0),
            D_O1: lambda: same(kind, k, mate, jo, 1),
            HALO: lambda: remote(kind, k, block(0, k, 0), block(ROW, k, 0), down),
            D_HALO: lambda: same(kind, k, mate, ROW, 0),
            HALO2: lambda: remote(kind, k, block(0, k, 1), block(ROW, k, 1), down),
        }[kind]()

    def recv(kind, k):
        return {
            RIGHT: lambda: same(kind, k, right, jl),
            LEFT: lambda: same(kind, k, left, jr),
            FWD_R: lambda: same(kind, k, right, jo, 0),
            FWD_L: lambda: same(kind, k, left, jo, 1),
            D_OWN: lambda: same(kind, k, mate, jp),
            D_L: lambda: same(kind, k, mate, ql),
            D_R: lambda: same(kind, k, mate, qr),
            D_O0: lambda: same(kind, k, mate, qo, 0),
            D_O1: lambda: same(kind, k, mate, qo, 1),
            HALO: lambda: same(kind, k, down, ROW, 0),
            D_HALO: lambda: same(kind, k, mate, ROW, 0),
            HALO2: lambda: same(kind, k, down, ROW, 1),
        }[kind]()

    def partial(kind, k):
        ys = pl.ds(OUTS[k], OUTS[k + 1] - OUTS[k])
        src, dst, peer = (Pm, Qm, up) if kind == UP else (P1, Q1, down)
        return remote(kind, k, src.at[:, ys], dst.at[:, ys], peer)

    def fill(k):
        lo, hi = CUTS[k], CUTS[k + 1]

        def put(row, src, y, to):
            C[row, to, pl.ds(0, 8), :] = src[pl.ds(24, 8), :]
            C[row, to, pl.ds(8, 32), :] = src[...]
            C[row, to, pl.ds(40, 8), :] = src[pl.ds(0, 8), :]

        def one(shift, row2):
            def step(y, _):
                rows = (RX + 1,) if row2 else range(RX + 1)
                for row in rows:
                    put(row, B.at[row // 2, row % 2, y], y, y + shift)
                return 0
            return step

        lax.fori_loop(lo, hi, one(0, False), 0)
        if k == 0:
            lax.fori_loop(0, LO + HI, one(NY, False), 0)

        @pl.when(last)
        def _():
            lax.fori_loop(lo, hi, one(0, True), 0)
            if k == 0:
                lax.fori_loop(0, LO + HI, one(NY, True), 0)

    def compute(k):
        lo, hi = OUTS[k], OUTS[k + 1]

        def tile(t, _):
            i = lax.rem(t, 2)
            t = lax.div(t, 2)
            z = lax.rem(t, NZ // (8 * ZT)) * (8 * ZT)
            y = lo + lax.div(t, NZ // (8 * ZT)) * G

            def control(u, acc):
                row = ip[i * NCTRL + u]
                yy = y + LO + ip[2 * NCTRL + u]
                zz = z + ip[3 * NCTRL + u]
                s1, s2 = ip[4 * NCTRL + u], ip[5 * NCTRL + u]
                f = [fp[q * NCTRL + u] for q in range(8)]
                c = [fp[(8 + 3 * i + e) * NCTRL + u] for e in range(3)]
                fields = []
                for q in range(G + 1):
                    low = f[0] * C[row, yy + q, pl.ds(zz, 8 * ZT), :] + f[1] * C[row, yy + q, pl.ds(zz + 1, 8 * ZT), :]
                    high = f[2] * C[row + 1, yy + q, pl.ds(zz, 8 * ZT), :] + f[3] * C[row + 1, yy + q, pl.ds(zz + 1, 8 * ZT), :]
                    fields.append(low + high)
                new = []
                for q in range(G):
                    h = f[4] * fields[q] + f[5] * fields[q + 1]
                    w = f[6] * pltpu.roll(h, s1, 1) + f[7] * pltpu.roll(h, s2, 1)
                    new += [jnp.minimum(acc[3 * q + e], w + c[e]) for e in range(3)]
                return tuple(new)

            start = tuple([jnp.full((8 * ZT, NW), jnp.inf, jnp.float32)] * (3 * G))
            acc = lax.fori_loop(0, NCTRL, control, start, unroll=True)
            zs = pl.ds(pl.multiple_of(z, 8), 8 * ZT)
            for q in range(G):
                for e, ref in enumerate((A, P1, Pm)):
                    ref[i, y + q, zs, :] = acc[3 * q + e]
            return 0

        lax.fori_loop(0, 2 * ((hi - lo) // G) * (NZ // (8 * ZT)), tile, 0)

    def combine(k):
        partial(UP, k).wait_recv()
        partial(DOWN, k).wait_recv()
        lo, hi = OUTS[k], OUTS[k + 1]

        def step(y, _):
            at = lax.rem(y + LO, NY)
            for i in range(2):
                best = jnp.minimum(A[i, y], jnp.minimum(Q1[i, y], Qm[i, y]))
                A[i, y] = jnp.maximum(O[i, at], jnp.minimum(T[i, at], best))
            return 0

        lax.fori_loop(lo, hi, step, 0)

    for k in range(min(2, STAGES)):
        send(RIGHT, k).start()
        send(LEFT, k).start()
    for k in range(STAGES):
        send(D_OWN, k).start()
    loads[1].start()
    loads[2].start()
    for k in range(STAGES):
        recv(RIGHT, k).wait_recv()
        send(FWD_R, k).start()
        send(D_L, k).start()
        recv(LEFT, k).wait_recv()
        send(FWD_L, k).start()
        send(D_R, k).start()
        if k + 2 < STAGES:
            send(RIGHT, k + 2).start()
            send(LEFT, k + 2).start()
        recv(FWD_R, k).wait_recv()
        send(D_O0, k).start()
        recv(FWD_L, k).wait_recv()
        send(D_O1, k).start()
        for kind in (D_OWN, D_L, D_R, D_O0, D_O1):
            recv(kind, k).wait_recv()

        @pl.when(core == 0)
        def _():
            send(HALO, k).start()

        @pl.when(last)
        def _():
            send(HALO2, k).start()

        @pl.when(core == 0)
        def _():
            recv(HALO, k).wait_recv()
            send(D_HALO, k).start()

        @pl.when(last)
        def _():
            recv(HALO2, k).wait_recv()

        @pl.when(core == 1)
        def _():
            recv(D_HALO, k).wait_recv()

        fill(k)
        compute(k)
        partial(UP, k).start()
        partial(DOWN, k).start()
        if k == 0:
            loads[1].wait()
            loads[2].wait()
        else:
            combine(k - 1)
    combine(STAGES - 1)

    stores = [pltpu.make_async_copy(A.at[:, pl.ds(0, NY - LO)], out.at[:, pl.ds(LO, NY - LO)], lsem.at[3]),
              pltpu.make_async_copy(A.at[:, pl.ds(NY - LO, LO)], out.at[:, pl.ds(0, LO)], lsem.at[4])]
    for copy in stores:
        copy.start()
    for k in range(STAGES):
        for kind in (RIGHT, LEFT, FWD_R, FWD_L, D_OWN, D_L, D_R, D_O0, D_O1):
            send(kind, k).wait_send()
        partial(UP, k).wait_send()
        partial(DOWN, k).wait_send()

        @pl.when(core == 0)
        def _():
            send(HALO, k).wait_send()
            send(D_HALO, k).wait_send()

        @pl.when(last)
        def _():
            send(HALO2, k).wait_send()

    for copy in stores:
        copy.wait()


def body(value, target, obstacle, fractions, control_cost, shard_offset, cell_offset, grid_offset):
    slab = (CX, NY, NZ, NW)
    vmem = functools.partial(pltpu.VMEM, dtype=jnp.float32)
    smem = pl.BlockSpec(memory_space=pltpu.SMEM)
    anywhere = pl.BlockSpec(memory_space=pl.ANY)
    return pl.pallas_call(
        kernel,
        name="reach_avoid",
        out_shape=jax.ShapeDtypeStruct(slab, jnp.float32),
        in_specs=[smem] * 5 + [anywhere] * 3,
        out_specs=anywhere,
        scratch_shapes=[
            vmem((ROW + 1,) + slab),
            vmem((RX + 2, NY + LO + HI, NZ + 16, NW)),
            vmem(slab), vmem(slab), vmem(slab), vmem(slab), vmem(slab), vmem(slab), vmem(slab),
            pltpu.SMEM((6 * NCTRL,), jnp.int32),
            pltpu.SMEM((14 * NCTRL,), jnp.float32),
            pltpu.SemaphoreType.DMA((KINDS, STAGES)),
            pltpu.SemaphoreType.DMA((KINDS, STAGES)),
            pltpu.SemaphoreType.DMA((5,)),
        ],
        compiler_params=pltpu.CompilerParams(collective_id=0, has_side_effects=True, vmem_limit_bytes=62 << 20),
    )(fractions, control_cost, shard_offset, cell_offset, grid_offset, value, target, obstacle)


def solution(mesh):
    grid = P("gx", None, None, None)
    return jax.shard_map(body, mesh=mesh, in_specs=(grid, grid, grid, P(), P(), P(), P(), P()), out_specs=grid,
                         check_vma=False)
```

time: 658 us -> 131 us (0.20)
  the two profiles are of different devices: /device:TPU:0 before, /device:TPU:1 now
where the time goes in v1:
time: 131 us
  Pallas kernels  125 us (95%)
  local copies, waits for them, and re-layouts  5.38 us (4%)
    pallas_call x1, Pallas kernels, body(): pl.pallas_call(kernel, name='reach_avoid', out_shape=jax.ShapeDtypeStruct...  125 us
    unnamed x3, local copies, waits for them, and re-layouts  5.38 us

profile of v1, /device:TPU:1, one launch (start us, length us, event | category | flops | bytes accessed | tf_op | source)
XLA Modules:
  0.0 130.9 jit_solution(17161456243638453673)
XLA Ops:
  0.0 1.4 %copy.9.frac = f32[16,4]{1,0:T(8,128)} copy(f32[16,4]{0,1:T(4,128)} %param.11) | data formatting | bytes 512 | tf_op args[3]
  1.4 1.4 %copy.10.go = s32[16,3]{1,0:T(8,128)} copy(s32[16,3]{0,1:T(4,128)} %param.15) | data formatting | bytes 384 | tf_op args[7]
  2.7 125.5 %reach_avoid.1 = f32[2,48,32,128]{3,2,1,0:T(8,128)} custom-call(f32[16,4]{1,0:T(8,128)} %copy.9.frac, f32[16]{0:T(128)} %cost.1, s32[16]{0:T(128)} %so.1, s32[16]{0:T(128)} %co.1, s32[16,3]{1,0:T(8,128)} %copy.10.go, f32[2,48,32,128]{3,2,1,0:T(8,128)} %value.1, f32[2,48,32,128]{3,2,1,0:T(8,128)} %target.1, f32[2,48,32,128]{3,2,1,0:T(8,128)} %obstacle.1), custom_call_target="tpu_custom_call" | custom-call | tf_op jit(solution)/shard_map/reach_avoid/pallas_call | solution.py:283
  128.2 2.7 %copy.12 = f32[2,48,32,128]{3,2,1,0:T(8,128)} copy(f32[2,48,32,128]{3,2,1,0:T(8,128)} %reach_avoid.1) | data formatting | bytes 3145728

commit v2 on v1

--- a/solution.py
+++ b/solution.py
@@ -11,18 +11,22 @@
 ROW = 8
 RX = ROW * CX
 LO, HI = 4, 5
-ENDS = (17, 29, 41, 48)
+ENDS = (13, 17, 21, 25, 29, 33, 37, 41, 45, 48)
+ORDER = tuple(zip("NNONOWNOWNOWNOWNOWNOWNONWOOWWW", (0, 1, 0, 2, 1, 0, 3, 2, 1, 4, 3, 2, 5, 4, 3, 6, 5, 4, 7, 6, 5, 8, 7, 9, 6, 8, 9, 7, 8, 9)))
+DEPTH = 2
 STAGES = len(ENDS)
 CUTS = (0,) + ENDS
 OUTS = (0,) + tuple(e - LO - HI for e in ENDS[:-1]) + (NY,)
 G, ZT = 4, 2
+PARTS = tuple((k, lo, OUTS[k + 1]) for k, lo in enumerate(OUTS[:-2])) + tuple(
+    (STAGES - 1, lo, lo + G) for lo in range(OUTS[-2], NY, G))
 MESH = pl.DeviceIdType.MESH
-(RIGHT, LEFT, FWD_R, FWD_L, D_OWN, D_L, D_R, D_O0, D_O1, HALO, D_HALO, HALO2, UP, DOWN) = range(14)
-KINDS = 14
+(RIGHT, LEFT, FWD_R, FWD_L, D_OWN, D_L, D_R, D_O0, D_O1, HALO, HALO_B, HALO2) = range(12)
+KINDS = 12
 
 
 def kernel(frac, cost, so, co, go, value, target, obstacle, out,
-           B, C, P1, Pm, Q1, Qm, A, T, O, ip, fp, ssem, rsem, lsem):
+           B, C, P1, Pm, Q1, Qm, A, T, O, ip, fp, ssem, rsem, psem, qsem, osem, lsem):
     n = lax.axis_size("gx")
     me = lax.axis_index("gx")
     j = lax.rem(me, ROW)
@@ -32,7 +36,9 @@
     qr, ql, qo = jr + 1 - 2 * core, jl + 1 - 2 * core, jo + 1 - 2 * core
     right, left, mate = base + jr, base + jl, base + jp
     up, down = lax.rem(me + ROW, n), lax.rem(me + n - ROW, n)
+    beyond = jnp.where(core == 0, down + 1, up - 1)
     last = j == ROW - 1
+    beside_last = j == ROW - 2
 
     loads = [pltpu.make_async_copy(value, B.at[j], lsem.at[0]),
              pltpu.make_async_copy(target, T, lsem.at[1]),
@@ -40,7 +46,7 @@
     loads[0].start()
 
     barrier = pltpu.get_barrier_semaphore()
-    for peer in (right, left, mate, up, down):
+    for peer in (right, left, mate, up, down, beyond):
         pl.semaphore_signal(barrier, inc=1, device_id=(peer,), device_id_type=MESH)
 
     def params(u, _):
@@ -51,11 +57,11 @@
             ip[i * NCTRL + u] = q - RX * d
             for e, which in enumerate((0, 1, -1)):
                 fp[(8 + 3 * i + e) * NCTRL + u] = jnp.where(d == which, cost[u], jnp.inf)
-        ip[2 * NCTRL + u] = go[u, 0]
-        ip[3 * NCTRL + u] = go[u, 1] + 8
-        ip[4 * NCTRL + u] = (NW - go[u, 2]) & (NW - 1)
-        ip[5 * NCTRL + u] = (NW - 1 - go[u, 2]) & (NW - 1)
-        f0, f1, f2, f3 = frac[u, 0], frac[u, 1], frac[u, 2], frac[u, 3]
+        ip[2 * NCTRL + u] = go[0, u]
+        ip[3 * NCTRL + u] = go[1, u] + 8
+        ip[4 * NCTRL + u] = (NW - go[2, u]) & (NW - 1)
+        ip[5 * NCTRL + u] = (NW - 1 - go[2, u]) & (NW - 1)
+        f0, f1, f2, f3 = frac[0, u], frac[1, u], frac[2, u], frac[3, u]
         fp[u] = (1.0 - f0) * (1.0 - f2)
         fp[NCTRL + u] = (1.0 - f0) * f2
         fp[2 * NCTRL + u] = f0 * (1.0 - f2)
@@ -68,7 +74,7 @@
 
     lax.fori_loop(0, NCTRL, params, 0)
     loads[0].wait()
-    pl.semaphore_wait(barrier, 5)
+    pl.semaphore_wait(barrier, 6)
 
     def remote(kind, k, src, dst, peer):
         return pltpu.make_async_remote_copy(src_ref=src, dst_ref=dst, send_sem=ssem.at[kind, k],
@@ -87,14 +93,14 @@
             LEFT: lambda: same(kind, k, left, j),
             FWD_R: lambda: same(kind, k, right, jl, 0),
             FWD_L: lambda: same(kind, k, left, jr, 1),
-            D_OWN: lambda: same(kind, k, mate, j),
+            D_OWN: lambda: remote(kind, k, B.at[j], B.at[j], mate),
             D_L: lambda: same(kind, k, mate, jl),
             D_R: lambda: same(kind, k, mate, jr),
             D_O0: lambda: same(kind, k, mate, jo, 0),
             D_O1: lambda: same(kind, k, mate, jo, 1),
             HALO: lambda: remote(kind, k, block(0, k, 0), block(ROW, k, 0), down),
-            D_HALO: lambda: same(kind, k, mate, ROW, 0),
-            HALO2: lambda: remote(kind, k, block(0, k, 1), block(ROW, k, 1), down),
+            HALO_B: lambda: remote(kind, k, block(0, k, 0), block(ROW, k, 0), beyond),
+            HALO2: lambda: remote(kind, k, block(0, k, 1), block(ROW, k, 1), beyond),
         }[kind]()
 
     def recv(kind, k):
@@ -103,20 +109,21 @@
             LEFT: lambda: same(kind, k, left, jr),
             FWD_R: lambda: same(kind, k, right, jo, 0),
             FWD_L: lambda: same(kind, k, left, jo, 1),
-            D_OWN: lambda: same(kind, k, mate, jp),
+            D_OWN: lambda: remote(kind, k, B.at[jp], B.at[jp], mate),
             D_L: lambda: same(kind, k, mate, ql),
             D_R: lambda: same(kind, k, mate, qr),
             D_O0: lambda: same(kind, k, mate, qo, 0),
             D_O1: lambda: same(kind, k, mate, qo, 1),
             HALO: lambda: same(kind, k, down, ROW, 0),
-            D_HALO: lambda: same(kind, k, mate, ROW, 0),
-            HALO2: lambda: same(kind, k, down, ROW, 1),
+            HALO_B: lambda: same(kind, k, beyond, ROW, 0),
+            HALO2: lambda: same(kind, k, beyond, ROW, 1),
         }[kind]()
 
-    def partial(kind, k):
-        ys = pl.ds(OUTS[k], OUTS[k + 1] - OUTS[k])
-        src, dst, peer = (Pm, Qm, up) if kind == UP else (P1, Q1, down)
-        return remote(kind, k, src.at[:, ys], dst.at[:, ys], peer)
+    def partial(kind, part):
+        ys = pl.ds(PARTS[part][1], PARTS[part][2] - PARTS[part][1])
+        src, dst, peer = (Pm, Qm, up) if kind == 0 else (P1, Q1, down)
+        return pltpu.make_async_remote_copy(src_ref=src.at[:, ys], dst_ref=dst.at[:, ys], send_sem=psem.at[kind, part],
+                                            recv_sem=qsem.at[kind, part], device_id=(peer,), device_id_type=MESH)
 
     def fill(k):
         lo, hi = CUTS[k], CUTS[k + 1]
@@ -144,8 +151,8 @@
             if k == 0:
                 lax.fori_loop(0, LO + HI, one(NY, True), 0)
 
-    def compute(k):
-        lo, hi = OUTS[k], OUTS[k + 1]
+    def compute(part):
+        _, lo, hi = PARTS[part]
 
         def tile(t, _):
             i = lax.rem(t, 2)
@@ -182,10 +189,10 @@
 
         lax.fori_loop(0, 2 * ((hi - lo) // G) * (NZ // (8 * ZT)), tile, 0)
 
-    def combine(k):
-        partial(UP, k).wait_recv()
-        partial(DOWN, k).wait_recv()
-        lo, hi = OUTS[k], OUTS[k + 1]
+    def combine(part):
+        partial(0, part).wait_recv()
+        partial(1, part).wait_recv()
+        _, lo, hi = PARTS[part]
 
         def step(y, _):
             at = lax.rem(y + LO, NY)
@@ -196,83 +203,117 @@
 
         lax.fori_loop(lo, hi, step, 0)
 
-    for k in range(min(2, STAGES)):
-        send(RIGHT, k).start()
-        send(LEFT, k).start()
-    for k in range(STAGES):
-        send(D_OWN, k).start()
-    loads[1].start()
-    loads[2].start()
-    for k in range(STAGES):
+    def own(k):
+        if k < STAGES:
+            send(RIGHT, k).start()
+            send(LEFT, k).start()
+
+    def halo(k, which):
+        @pl.when(which)
+        def _():
+            send(HALO, k).start()
+            send(HALO_B, k).start()
+
+    def neighbours(k):
         recv(RIGHT, k).wait_recv()
         send(FWD_R, k).start()
         send(D_L, k).start()
+        halo(k, j == 2)
         recv(LEFT, k).wait_recv()
         send(FWD_L, k).start()
         send(D_R, k).start()
-        if k + 2 < STAGES:
-            send(RIGHT, k + 2).start()
-            send(LEFT, k + 2).start()
+        halo(k, j == 6)
+
+        @pl.when(beside_last)
+        def _():
+            send(HALO2, k).start()
+
+        own(k + DEPTH)
+
+    def opposite(k):
         recv(FWD_R, k).wait_recv()
         send(D_O0, k).start()
+        halo(k, j == 4)
         recv(FWD_L, k).wait_recv()
         send(D_O1, k).start()
-        for kind in (D_OWN, D_L, D_R, D_O0, D_O1):
+
+    def work(k):
+        if k == 0:
+            recv(D_OWN, 0).wait_recv()
+        for kind in (D_L, D_R, D_O0, D_O1):
             recv(kind, k).wait_recv()
 
         @pl.when(core == 0)
         def _():
-            send(HALO, k).start()
+            recv(HALO, k).wait_recv()
+
+        @pl.when(core == 1)
+        def _():
+            recv(HALO_B, k).wait_recv()
 
         @pl.when(last)
         def _():
-            send(HALO2, k).start()
+            recv(HALO2, k).wait_recv()
+
+        fill(k)
+        for part, (stage, _, _) in enumerate(PARTS):
+            if stage == k:
+                compute(part)
+                partial(0, part).start()
+                partial(1, part).start()
+
+    def store(part):
+        _, lo, hi = PARTS[part]
+        return pltpu.make_async_copy(A.at[:, pl.ds(lo, hi - lo)], out.at[:, pl.ds((lo + LO) % NY, hi - lo)],
+                                     osem.at[part])
+
+    def finish(stage):
+        for part, (k, _, _) in enumerate(PARTS):
+            if k == stage:
+                combine(part)
+                store(part).start()
+
+    for k in range(DEPTH):
+        own(k)
+    send(D_OWN, 0).start()
+    for k in range(STAGES):
+        halo(k, j == 0)
+    loads[1].start()
+    loads[2].start()
+    for what, k in ORDER:
+        if what == "N":
+            neighbours(k)
+        elif what == "O":
+            opposite(k)
+        else:
+            work(k)
+            if k == 1:
+                loads[1].wait()
+                loads[2].wait()
+            if k >= 2:
+                finish(k - 2)
+    finish(STAGES - 2)
+    finish(STAGES - 1)
+
+    send(D_OWN, 0).wait_send()
+    for k in range(STAGES):
+        for kind in (RIGHT, LEFT, FWD_R, FWD_L, D_L, D_R, D_O0, D_O1):
+            send(kind, k).wait_send()
 
         @pl.when(core == 0)
         def _():
-            recv(HALO, k).wait_recv()
-            send(D_HALO, k).start()
-
-        @pl.when(last)
-        def _():
-            recv(HALO2, k).wait_recv()
-
-        @pl.when(core == 1)
-        def _():
-            recv(D_HALO, k).wait_recv()
-
-        fill(k)
-        compute(k)
-        partial(UP, k).start()
-        partial(DOWN, k).start()
-        if k == 0:
-            loads[1].wait()
-            loads[2].wait()
-        else:
-            combine(k - 1)
-    combine(STAGES - 1)
-
-    stores = [pltpu.make_async_copy(A.at[:, pl.ds(0, NY - LO)], out.at[:, pl.ds(LO, NY - LO)], lsem.at[3]),
-              pltpu.make_async_copy(A.at[:, pl.ds(NY - LO, LO)], out.at[:, pl.ds(0, LO)], lsem.at[4])]
-    for copy in stores:
-        copy.start()
-    for k in range(STAGES):
-        for kind in (RIGHT, LEFT, FWD_R, FWD_L, D_OWN, D_L, D_R, D_O0, D_O1):
-            send(kind, k).wait_send()
-        partial(UP, k).wait_send()
-        partial(DOWN, k).wait_send()
-
-        @pl.when(core == 0)
-        def _():
             send(HALO, k).wait_send()
-            send(D_HALO, k).wait_send()
-
-        @pl.when(last)
+            send(HALO_B, k).wait_send()
+
+        @pl.when(beside_last)
         def _():
             send(HALO2, k).wait_send()
 
-    for copy in stores:
-        copy.wait()
+    for part in range(len(PARTS)):
+        partial(0, part).wait_send()
+        partial(1, part).wait_send()
+    for part in range(len(PARTS)):
+        store(part).wait()
 
 
 def body(value, target, obstacle, fractions, control_cost, shard_offset, cell_offset, grid_offset):
@@ -294,10 +335,13 @@
             pltpu.SMEM((14 * NCTRL,), jnp.float32),
             pltpu.SemaphoreType.DMA((KINDS, STAGES)),
             pltpu.SemaphoreType.DMA((KINDS, STAGES)),
-            pltpu.SemaphoreType.DMA((5,)),
+            pltpu.SemaphoreType.DMA((2, len(PARTS))),
+            pltpu.SemaphoreType.DMA((2, len(PARTS))),
+            pltpu.SemaphoreType.DMA((len(PARTS),)),
+            pltpu.SemaphoreType.DMA((3,)),
         ],
         compiler_params=pltpu.CompilerParams(collective_id=0, has_side_effects=True, vmem_limit_bytes=62 << 20),
-    )(fractions, control_cost, shard_offset, cell_offset, grid_offset, value, target, obstacle)
+    )(fractions.T, control_cost, shard_offset, cell_offset, grid_offset.T, value, target, obstacle)
 
 
 def solution(mesh):

time: 131 us -> 91.8 us (0.70)
  the two profiles are of different devices: /device:TPU:1 before, /device:TPU:6 now
where the time goes in v2:
time: 91.8 us; the launch traced here: 91.7 us
  Pallas kernels  89 us (97%)
  local copies, waits for them, and re-layouts  2.67 us (3%)
    pallas_call x1, Pallas kernels, body(): pl.pallas_call(kernel, name='reach_avoid', out_shape=jax.ShapeDtypeStruct...  89 us
    unnamed x1, local copies, waits for them, and re-layouts  2.67 us

profile of v2, /device:TPU:6, one launch (start us, length us, event | category | flops | bytes accessed | tf_op | source)
XLA Modules:
  0.0 91.7 jit_solution(10338532401735113306)
XLA Ops:
  0.0 89.0 %reach_avoid.1 = f32[2,48,32,128]{3,2,1,0:T(8,128)} custom-call(f32[4,16]{1,0:T(4,128)} %bitcast.2, f32[16]{0:T(128)} %cost.1, s32[16]{0:T(128)} %so.1, s32[16]{0:T(128)} %co.1, s32[3,16]{1,0:T(4,128)} %bitcast.3, f32[2,48,32,128]{3,2,1,0:T(8,128)} %value.1, f32[2,48,32,128]{3,2,1,0:T(8,128)} %target.1, f32[2,48,32,128]{3,2,1,0:T(8,128)} %obstacle.1), custom_call_target="tpu_custom_call" | custom-call | tf_op jit(solution)/shard_map/reach_avoid/pallas_call | solution.py:324
  89.0 2.7 %copy.10 = f32[2,48,32,128]{3,2,1,0:T(8,128)} copy(f32[2,48,32,128]{3,2,1,0:T(8,128)} %reach_avoid.1) | data formatting | bytes 3145728

commit v3 on v2

--- a/solution.py
+++ b/solution.py
@@ -12,7 +12,8 @@
 RX = ROW * CX
 LO, HI = 4, 5
 ENDS = (13, 17, 21, 25, 29, 33, 37, 41, 45, 48)
-ORDER = tuple(zip("NNONOWNOWNOWNOWNOWNOWNONWOOWWW", (0, 1, 0, 2, 1, 0, 3, 2, 1, 4, 3, 2, 5, 4, 3, 6, 5, 4, 7, 6, 5, 8, 7, 9, 6, 8, 9, 7, 8, 9)))
+ORDER = tuple(zip("NNONHOWNHOWNHOWNHOWNHOWNHOWNHONWOHOWHHWW", (0, 1, 0, 2, 0, 1, 0, 3, 1, 2, 1, 4, 2, 3, 2, 5, 3, 4, 3, 6, 4, 5, 4, 7, 5, 6, 5, 8, 6, 7, 9, 6, 8, 7, 9, 7, 8, 9, 8, 9)))
+LAG = 5
 DEPTH = 2
 STAGES = len(ENDS)
 CUTS = (0,) + ENDS
@@ -21,12 +22,12 @@
 PARTS = tuple((k, lo, OUTS[k + 1]) for k, lo in enumerate(OUTS[:-2])) + tuple(
     (STAGES - 1, lo, lo + G) for lo in range(OUTS[-2], NY, G))
 MESH = pl.DeviceIdType.MESH
-(RIGHT, LEFT, FWD_R, FWD_L, D_OWN, D_L, D_R, D_O0, D_O1, HALO, HALO_B, HALO2) = range(12)
+(RIGHT, LEFT, FWD_R, FWD_L, D_OWN, D_L, D_R, D_O0, D_O1, HALO, D_HALO, HALO2) = range(12)
 KINDS = 12
 
 
 def kernel(frac, cost, so, co, go, value, target, obstacle, out,
-           B, C, P1, Pm, Q1, Qm, A, T, O, ip, fp, ssem, rsem, psem, qsem, osem, lsem):
+           B, C, P1, Pm, Q1, Qm, A, T, O, R, ip, fp, ssem, rsem, psem, qsem, osem, lsem):
     n = lax.axis_size("gx")
     me = lax.axis_index("gx")
     j = lax.rem(me, ROW)
@@ -49,32 +50,49 @@
     for peer in (right, left, mate, up, down, beyond):
         pl.semaphore_signal(barrier, inc=1, device_id=(peer,), device_id_type=MESH)
 
-    def params(u, _):
+    loads[0].wait()
+    pl.semaphore_wait(barrier, 6)
+
+    def rank(u, _):
+        mine = 2 * so[u] + co[u]
+        before = 0
+        for v in range(NCTRL):
+            other = 2 * so[v] + co[v]
+            before += jnp.where((other > mine) | ((other == mine) & (v < u)), 1, 0)
+        ip[9 * NCTRL + u] = before
+        return 0
+
+    def params(k, _):
+        u = 0
+        for v in range(NCTRL):
+            u += jnp.where(ip[9 * NCTRL + v] == k, v, 0)
         off = 2 * so[u] + co[u]
         for i in range(2):
             q = 2 * j + i + off
             d = jnp.where(q < 0, -1, jnp.where(q < RX, 0, 1))
-            ip[i * NCTRL + u] = q - RX * d
-            for e, which in enumerate((0, 1, -1)):
-                fp[(8 + 3 * i + e) * NCTRL + u] = jnp.where(d == which, cost[u], jnp.inf)
-        ip[2 * NCTRL + u] = go[0, u]
-        ip[3 * NCTRL + u] = go[1, u] + 8
-        ip[4 * NCTRL + u] = (NW - go[2, u]) & (NW - 1)
-        ip[5 * NCTRL + u] = (NW - 1 - go[2, u]) & (NW - 1)
+            before = ip[(6 + i) * NCTRL]
+            ip[i * NCTRL + k] = q - RX * d
+            fresh = (k == 0) | (d != before)
+            fp[(9 + i) * NCTRL + k] = jnp.where(fresh, jnp.inf, -jnp.inf)
+            ip[(6 + i) * NCTRL] = d
+            for e in (1, 2, 3):
+                at = (6 + i) * NCTRL + e
+                ip[at] = jnp.where(d == 2 - e, k, jnp.where(k == 0, NCTRL, ip[at]))
+        ip[2 * NCTRL + k] = go[0, u]
+        ip[3 * NCTRL + k] = go[1, u] + 8
+        ip[4 * NCTRL + k] = (NW - go[2, u]) & (NW - 1)
+        ip[5 * NCTRL + k] = (NW - 1 - go[2, u]) & (NW - 1)
         f0, f1, f2, f3 = frac[0, u], frac[1, u], frac[2, u], frac[3, u]
-        fp[u] = (1.0 - f0) * (1.0 - f2)
-        fp[NCTRL + u] = (1.0 - f0) * f2
-        fp[2 * NCTRL + u] = f0 * (1.0 - f2)
-        fp[3 * NCTRL + u] = f0 * f2
-        fp[4 * NCTRL + u] = 1.0 - f1
-        fp[5 * NCTRL + u] = f1
-        fp[6 * NCTRL + u] = 1.0 - f3
-        fp[7 * NCTRL + u] = f3
+        fp[k] = (1.0 - f0) * (1.0 - f2)
+        fp[NCTRL + k] = (1.0 - f0) * f2
+        fp[2 * NCTRL + k] = f0 * (1.0 - f2)
+        fp[3 * NCTRL + k] = f0 * f2
+        fp[4 * NCTRL + k] = 1.0 - f1
+        fp[5 * NCTRL + k] = f1
+        fp[6 * NCTRL + k] = 1.0 - f3
+        fp[7 * NCTRL + k] = f3
+        fp[8 * NCTRL + k] = cost[u]
         return 0
-
-    lax.fori_loop(0, NCTRL, params, 0)
-    loads[0].wait()
-    pl.semaphore_wait(barrier, 6)
 
     def remote(kind, k, src, dst, peer):
         return pltpu.make_async_remote_copy(src_ref=src, dst_ref=dst, send_sem=ssem.at[kind, k],
@@ -99,7 +117,7 @@
             D_O0: lambda: same(kind, k, mate, jo, 0),
             D_O1: lambda: same(kind, k, mate, jo, 1),
             HALO: lambda: remote(kind, k, block(0, k, 0), block(ROW, k, 0), down),
-            HALO_B: lambda: remote(kind, k, block(0, k, 0), block(ROW, k, 0), beyond),
+            D_HALO: lambda: same(kind, k, mate, ROW, 0),
             HALO2: lambda: remote(kind, k, block(0, k, 1), block(ROW, k, 1), beyond),
         }[kind]()
 
@@ -115,7 +133,7 @@
             D_O0: lambda: same(kind, k, mate, qo, 0),
             D_O1: lambda: same(kind, k, mate, qo, 1),
             HALO: lambda: same(kind, k, down, ROW, 0),
-            HALO_B: lambda: same(kind, k, beyond, ROW, 0),
+            D_HALO: lambda: same(kind, k, mate, ROW, 0),
             HALO2: lambda: same(kind, k, beyond, ROW, 1),
         }[kind]()
 
@@ -166,7 +184,7 @@
                 zz = z + ip[3 * NCTRL + u]
                 s1, s2 = ip[4 * NCTRL + u], ip[5 * NCTRL + u]
                 f = [fp[q * NCTRL + u] for q in range(8)]
-                c = [fp[(8 + 3 * i + e) * NCTRL + u] for e in range(3)]
+                c, fresh = fp[8 * NCTRL + u], fp[(9 + i) * NCTRL + u]
                 fields = []
                 for q in range(G + 1):
                     low = f[0] * C[row, yy + q, pl.ds(zz, 8 * ZT), :] + f[1] * C[row, yy + q, pl.ds(zz + 1, 8 * ZT), :]
@@ -176,15 +194,16 @@
                 for q in range(G):
                     h = f[4] * fields[q] + f[5] * fields[q + 1]
                     w = f[6] * pltpu.roll(h, s1, 1) + f[7] * pltpu.roll(h, s2, 1)
-                    new += [jnp.minimum(acc[3 * q + e], w + c[e]) for e in range(3)]
+                    new.append(jnp.minimum(jnp.maximum(acc[q], fresh), w + c))
+                    R[u, q] = new[q]
                 return tuple(new)
 
-            start = tuple([jnp.full((8 * ZT, NW), jnp.inf, jnp.float32)] * (3 * G))
-            acc = lax.fori_loop(0, NCTRL, control, start, unroll=True)
+            start = tuple([jnp.full((8 * ZT, NW), jnp.inf, jnp.float32)] * G)
+            lax.fori_loop(0, NCTRL, control, start, unroll=True)
             zs = pl.ds(pl.multiple_of(z, 8), 8 * ZT)
             for q in range(G):
-                for e, ref in enumerate((A, P1, Pm)):
-                    ref[i, y + q, zs, :] = acc[3 * q + e]
+                for e, ref in ((1, P1), (2, A), (3, Pm)):
+                    ref[i, y + q, zs, :] = R[ip[(6 + i) * NCTRL + e], q]
             return 0
 
         lax.fori_loop(0, 2 * ((hi - lo) // G) * (NZ // (8 * ZT)), tile, 0)
@@ -212,7 +231,6 @@
         @pl.when(which)
         def _():
             send(HALO, k).start()
-            send(HALO_B, k).start()
 
     def neighbours(k):
         recv(RIGHT, k).wait_recv()
@@ -237,19 +255,21 @@
         recv(FWD_L, k).wait_recv()
         send(D_O1, k).start()
 
+    def pass_halo(k):
+        @pl.when(core == 0)
+        def _():
+            recv(HALO, k).wait_recv()
+            send(D_HALO, k).start()
+
     def work(k):
         if k == 0:
             recv(D_OWN, 0).wait_recv()
         for kind in (D_L, D_R, D_O0, D_O1):
             recv(kind, k).wait_recv()
 
-        @pl.when(core == 0)
-        def _():
-            recv(HALO, k).wait_recv()
-
         @pl.when(core == 1)
         def _():
-            recv(HALO_B, k).wait_recv()
+            recv(D_HALO, k).wait_recv()
 
         @pl.when(last)
         def _():
@@ -272,6 +292,21 @@
             if k == stage:
                 combine(part)
                 store(part).start()
+
+    def drain():
+        send(D_OWN, 0).wait_send()
+        for k in range(STAGES):
+            for kind in (RIGHT, LEFT, FWD_R, FWD_L, D_L, D_R, D_O0, D_O1):
+                send(kind, k).wait_send()
+
+            @pl.when(core == 0)
+            def _():
+                send(HALO, k).wait_send()
+                send(D_HALO, k).wait_send()
+
+            @pl.when(beside_last)
+            def _():
+                send(HALO2, k).wait_send()
 
     for k in range(DEPTH):
         own(k)
@@ -280,34 +315,30 @@
         halo(k, j == 0)
     loads[1].start()
     loads[2].start()
+    R[NCTRL] = jnp.full(R.shape[1:], jnp.inf, jnp.float32)
+    for i in range(2):
+        ip[(6 + i) * NCTRL] = 0
+        for e in (1, 2, 3):
+            ip[(6 + i) * NCTRL + e] = 0
+    lax.fori_loop(0, NCTRL, rank, 0)
+    lax.fori_loop(0, NCTRL, params, 0)
     for what, k in ORDER:
         if what == "N":
             neighbours(k)
         elif what == "O":
             opposite(k)
+        elif what == "H":
+            pass_halo(k)
         else:
             work(k)
             if k == 1:
                 loads[1].wait()
                 loads[2].wait()
-            if k >= 2:
-                finish(k - 2)
-    finish(STAGES - 2)
-    finish(STAGES - 1)
-
-    send(D_OWN, 0).wait_send()
-    for k in range(STAGES):
-        for kind in (RIGHT, LEFT, FWD_R, FWD_L, D_L, D_R, D_O0, D_O1):
-            send(kind, k).wait_send()
-
-        @pl.when(core == 0)
-        def _():
-            send(HALO, k).wait_send()
-            send(HALO_B, k).wait_send()
-
-        @pl.when(beside_last)
-        def _():
-            send(HALO2, k).wait_send()
+            if k >= LAG:
+                finish(k - LAG)
+    drain()
+    for k in range(STAGES - LAG, STAGES):
+        finish(k)
 
     for part in range(len(PARTS)):
         partial(0, part).wait_send()
@@ -331,8 +362,9 @@
             vmem((ROW + 1,) + slab),
             vmem((RX + 2, NY + LO + HI, NZ + 16, NW)),
             vmem(slab), vmem(slab), vmem(slab), vmem(slab), vmem(slab), vmem(slab), vmem(slab),
-            pltpu.SMEM((6 * NCTRL,), jnp.int32),
-            pltpu.SMEM((14 * NCTRL,), jnp.float32),
+            vmem((NCTRL + 1, G, 8 * ZT, NW)),
+            pltpu.SMEM((10 * NCTRL,), jnp.int32),
+            pltpu.SMEM((11 * NCTRL,), jnp.float32),
             pltpu.SemaphoreType.DMA((KINDS, STAGES)),
             pltpu.SemaphoreType.DMA((KINDS, STAGES)),
             pltpu.SemaphoreType.DMA((2, len(PARTS))),

time: 91.8 us -> 89.8 us (0.978)
  the two profiles are of different devices: /device:TPU:6 before, /device:TPU:1 now
where the time goes in v3:
time: 89.8 us; the launch traced here: 88.4 us
  Pallas kernels  85.7 us (95%)
  local copies, waits for them, and re-layouts  2.67 us (3%)
    pallas_call x1, Pallas kernels, body(): pl.pallas_call(kernel, name='reach_avoid', out_shape=jax.ShapeDtypeStruct...  85.7 us
    unnamed x1, local copies, waits for them, and re-layouts  2.67 us

profile of v3, /device:TPU:1, one launch (start us, length us, event | category | flops | bytes accessed | tf_op | source)
XLA Modules:
  0.0 88.4 jit_solution(17706532038902987683)
XLA Ops:
  0.0 85.7 %reach_avoid.1 = f32[2,48,32,128]{3,2,1,0:T(8,128)} custom-call(f32[4,16]{1,0:T(4,128)} %bitcast.2, f32[16]{0:T(128)} %cost.1, s32[16]{0:T(128)} %so.1, s32[16]{0:T(128)} %co.1, s32[3,16]{1,0:T(4,128)} %bitcast.3, f32[2,48,32,128]{3,2,1,0:T(8,128)} %value.1, f32[2,48,32,128]{3,2,1,0:T(8,128)} %target.1, f32[2,48,32,128]{3,2,1,0:T(8,128)} %obstacle.1), custom_call_target="tpu_custom_call" | custom-call | tf_op jit(solution)/shard_map/reach_avoid/pallas_call | solution.py:355
  85.7 2.7 %copy.10 = f32[2,48,32,128]{3,2,1,0:T(8,128)} copy(f32[2,48,32,128]{3,2,1,0:T(8,128)} %reach_avoid.1) | data formatting | bytes 3145728

commit v4 on v3

--- a/solution.py
+++ b/solution.py
@@ -12,7 +12,7 @@
 RX = ROW * CX
 LO, HI = 4, 5
 ENDS = (13, 17, 21, 25, 29, 33, 37, 41, 45, 48)
-ORDER = tuple(zip("NNONHOWNHOWNHOWNHOWNHOWNHOWNHONWOHOWHHWW", (0, 1, 0, 2, 0, 1, 0, 3, 1, 2, 1, 4, 2, 3, 2, 5, 3, 4, 3, 6, 4, 5, 4, 7, 5, 6, 5, 8, 6, 7, 9, 6, 8, 7, 9, 7, 8, 9, 8, 9)))
+ORDER = tuple(zip("NNONOHWNOHWNOHWNOHWNOHWNOHWNWOHNWOHWOHW", (0, 1, 0, 2, 1, 0, 0, 3, 2, 1, 1, 4, 3, 2, 2, 5, 4, 3, 3, 6, 5, 4, 4, 7, 6, 5, 5, 8, 6, 7, 6, 9, 7, 8, 7, 8, 9, 8, 9)))
 LAG = 5
 DEPTH = 2
 STAGES = len(ENDS)
@@ -22,12 +22,14 @@
 PARTS = tuple((k, lo, OUTS[k + 1]) for k, lo in enumerate(OUTS[:-2])) + tuple(
     (STAGES - 1, lo, lo + G) for lo in range(OUTS[-2], NY, G))
 MESH = pl.DeviceIdType.MESH
-(RIGHT, LEFT, FWD_R, FWD_L, D_OWN, D_L, D_R, D_O0, D_O1, HALO, D_HALO, HALO2) = range(12)
-KINDS = 12
-
+SPANS = tuple((ENDS[min(k, STAGES - 1)] if k else 0, ENDS[min(k + 1, STAGES - 1)]) for k in range(STAGES))
+SPANS = (SPANS, tuple(zip(CUTS[:-1], CUTS[1:])))
+MOVED = tuple(SPANS[0][k][1] - SPANS[0][k][0] + CUTS[k + 1] - CUTS[k] for k in range(STAGES))
+(RIGHT, LEFT, FWD_R, FWD_L, D_OWN, D_L, D_R, D_O, HALO, D_HALO, HALO2, D_HALO2, PART, STORE) = range(14)
+(A_RIGHT, A_LEFT, A_FWD, A_D, A_HALO, A_D_HALO, A_HALO2, A_D_HALO2) = range(8)
 
 def kernel(frac, cost, so, co, go, value, target, obstacle, out,
-           B, C, P1, Pm, Q1, Qm, A, T, O, R, ip, fp, ssem, rsem, psem, qsem, osem, lsem):
+           B, C, P1, Pm, Q1, Qm, A, T, O, R, ip, fp, ssem, rsem, qsem, lsem, ysem):
     n = lax.axis_size("gx")
     me = lax.axis_index("gx")
     j = lax.rem(me, ROW)
@@ -37,7 +39,6 @@
     qr, ql, qo = jr + 1 - 2 * core, jl + 1 - 2 * core, jo + 1 - 2 * core
     right, left, mate = base + jr, base + jl, base + jp
     up, down = lax.rem(me + ROW, n), lax.rem(me + n - ROW, n)
-    beyond = jnp.where(core == 0, down + 1, up - 1)
     last = j == ROW - 1
     beside_last = j == ROW - 2
 
@@ -47,11 +48,12 @@
     loads[0].start()
 
     barrier = pltpu.get_barrier_semaphore()
-    for peer in (right, left, mate, up, down, beyond):
+    for peer in (right, left, mate, down):
         pl.semaphore_signal(barrier, inc=1, device_id=(peer,), device_id_type=MESH)
 
     loads[0].wait()
-    pl.semaphore_wait(barrier, 6)
+    pl.semaphore_wait(barrier, 4)
+    pl.semaphore_signal(ysem, inc=1, device_id=(up,), device_id_type=MESH)
 
     def rank(u, _):
         mine = 2 * so[u] + co[u]
@@ -94,54 +96,30 @@
         fp[8 * NCTRL + k] = cost[u]
         return 0
 
-    def remote(kind, k, src, dst, peer):
-        return pltpu.make_async_remote_copy(src_ref=src, dst_ref=dst, send_sem=ssem.at[kind, k],
-                                            recv_sem=rsem.at[kind, k], device_id=(peer,), device_id_type=MESH)
-
-    def block(slab, k, row=None):
-        ys = pl.ds(CUTS[k], CUTS[k + 1] - CUTS[k])
-        return B.at[slab, :, ys] if row is None else B.at[slab, row, ys]
-
-    def same(kind, k, peer, slab, row=None):
-        return remote(kind, k, block(slab, k, row), block(slab, k, row), peer)
-
-    def send(kind, k):
-        return {
-            RIGHT: lambda: same(kind, k, right, j),
-            LEFT: lambda: same(kind, k, left, j),
-            FWD_R: lambda: same(kind, k, right, jl, 0),
-            FWD_L: lambda: same(kind, k, left, jr, 1),
-            D_OWN: lambda: remote(kind, k, B.at[j], B.at[j], mate),
-            D_L: lambda: same(kind, k, mate, jl),
-            D_R: lambda: same(kind, k, mate, jr),
-            D_O0: lambda: same(kind, k, mate, jo, 0),
-            D_O1: lambda: same(kind, k, mate, jo, 1),
-            HALO: lambda: remote(kind, k, block(0, k, 0), block(ROW, k, 0), down),
-            D_HALO: lambda: same(kind, k, mate, ROW, 0),
-            HALO2: lambda: remote(kind, k, block(0, k, 1), block(ROW, k, 1), beyond),
-        }[kind]()
-
-    def recv(kind, k):
-        return {
-            RIGHT: lambda: same(kind, k, right, jl),
-            LEFT: lambda: same(kind, k, left, jr),
-            FWD_R: lambda: same(kind, k, right, jo, 0),
-            FWD_L: lambda: same(kind, k, left, jo, 1),
-            D_OWN: lambda: remote(kind, k, B.at[jp], B.at[jp], mate),
-            D_L: lambda: same(kind, k, mate, ql),
-            D_R: lambda: same(kind, k, mate, qr),
-            D_O0: lambda: same(kind, k, mate, qo, 0),
-            D_O1: lambda: same(kind, k, mate, qo, 1),
-            HALO: lambda: same(kind, k, down, ROW, 0),
-            D_HALO: lambda: same(kind, k, mate, ROW, 0),
-            HALO2: lambda: same(kind, k, beyond, ROW, 1),
-        }[kind]()
-
-    def partial(kind, part):
-        ys = pl.ds(PARTS[part][1], PARTS[part][2] - PARTS[part][1])
-        src, dst, peer = (Pm, Qm, up) if kind == 0 else (P1, Q1, down)
-        return pltpu.make_async_remote_copy(src_ref=src.at[:, ys], dst_ref=dst.at[:, ys], send_sem=psem.at[kind, part],
-                                            recv_sem=qsem.at[kind, part], device_id=(peer,), device_id_type=MESH)
+    def remote(out_sem, in_sem, src, dst, peer):
+        return pltpu.make_async_remote_copy(src_ref=src, dst_ref=dst, send_sem=out_sem, recv_sem=in_sem,
+                                            device_id=(peer,), device_id_type=MESH)
+
+    def move(kind, arrival, k, peer, slab, rows, to=None):
+        for row in rows:
+            lo, hi = SPANS[row][k]
+            if lo < hi:
+                ys = pl.ds(lo, hi - lo)
+                remote(ssem.at[kind], rsem.at[arrival, k], B.at[slab, row, ys],
+                       B.at[slab if to is None else to, row, ys], peer).start()
+
+    def arrived(arrival, k, peer, cells, slabs=1):
+        some = B.at[pl.ds(0, slabs), 0, pl.ds(0, cells)]
+        remote(ssem.at[RIGHT], rsem.at[arrival, k], some, some, peer).wait_recv()
+
+    def sent(kind, ref):
+        remote(ssem.at[kind], rsem.at[A_RIGHT, 0], ref, ref, right).wait_send()
+
+    def partials(part):
+        _, lo, hi = PARTS[part]
+        ys = pl.ds(lo, hi - lo)
+        for src, dst, peer in ((Pm, Qm, up), (P1, Q1, down)):
+            remote(ssem.at[PART], qsem.at[part], src.at[:, ys], dst.at[:, ys], peer).start()
 
     def fill(k):
         lo, hi = CUTS[k], CUTS[k + 1]
@@ -209,9 +187,9 @@
         lax.fori_loop(0, 2 * ((hi - lo) // G) * (NZ // (8 * ZT)), tile, 0)
 
     def combine(part):
-        partial(0, part).wait_recv()
-        partial(1, part).wait_recv()
         _, lo, hi = PARTS[part]
+        some = Q1.at[:, pl.ds(0, 2 * (hi - lo))]
+        remote(ssem.at[PART], qsem.at[part], some, some, down).wait_recv()
 
         def step(y, _):
             at = lax.rem(y + LO, NY)
@@ -224,68 +202,75 @@
 
     def own(k):
         if k < STAGES:
-            send(RIGHT, k).start()
-            send(LEFT, k).start()
+            move(RIGHT, A_RIGHT, k, right, j, (0, 1))
+            move(LEFT, A_LEFT, k, left, j, (0, 1))
 
     def halo(k, which):
         @pl.when(which)
         def _():
-            send(HALO, k).start()
+            move(HALO, A_HALO, k, down, 0, (0,), ROW)
 
     def neighbours(k):
-        recv(RIGHT, k).wait_recv()
-        send(FWD_R, k).start()
-        send(D_L, k).start()
+        arrived(A_RIGHT, k, right, MOVED[k])
+        move(FWD_R, A_FWD, k, right, jl, (0,))
+        move(D_L, A_D, k, mate, jl, (0, 1))
+        if k == 0:
+            pl.semaphore_wait(ysem, 1)
+            for early in range(STAGES):
+                halo(early, j == 0)
         halo(k, j == 2)
-        recv(LEFT, k).wait_recv()
-        send(FWD_L, k).start()
-        send(D_R, k).start()
-        halo(k, j == 6)
+        arrived(A_LEFT, k, left, MOVED[k])
+        move(FWD_L, A_FWD, k, left, jr, (1,))
+        move(D_R, A_D, k, mate, jr, (0, 1))
+        halo(k, beside_last)
 
         @pl.when(beside_last)
         def _():
-            send(HALO2, k).start()
+            move(HALO2, A_HALO2, k, down, 0, (1,), ROW)
 
         own(k + DEPTH)
 
     def opposite(k):
-        recv(FWD_R, k).wait_recv()
-        send(D_O0, k).start()
+        arrived(A_FWD, k, right, MOVED[k])
         halo(k, j == 4)
-        recv(FWD_L, k).wait_recv()
-        send(D_O1, k).start()
+        move(D_O, A_D, k, mate, jo, (0, 1))
 
     def pass_halo(k):
         @pl.when(core == 0)
         def _():
-            recv(HALO, k).wait_recv()
-            send(D_HALO, k).start()
+            arrived(A_HALO, k, down, SPANS[0][k][1] - SPANS[0][k][0])
+            move(D_HALO, A_D_HALO, k, mate, ROW, (0,))
 
     def work(k):
+        @pl.when(beside_last)
+        def _():
+            arrived(A_HALO2, k, down, CUTS[k + 1] - CUTS[k])
+            move(D_HALO2, A_D_HALO2, k, mate, ROW, (1,))
+
         if k == 0:
-            recv(D_OWN, 0).wait_recv()
-        for kind in (D_L, D_R, D_O0, D_O1):
-            recv(kind, k).wait_recv()
-
-        @pl.when(core == 1)
-        def _():
-            recv(D_HALO, k).wait_recv()
+            remote(ssem.at[D_OWN], rsem.at[A_D, STAGES], B.at[jp], B.at[jp], mate).wait_recv()
+        arrived(A_D, k, mate, MOVED[k], 3)
+        if k != 1:
+            ahead = max(k - 1, 0)
+
+            @pl.when(core == 1)
+            def _():
+                arrived(A_D_HALO, ahead, mate, SPANS[0][ahead][1] - SPANS[0][ahead][0])
 
         @pl.when(last)
         def _():
-            recv(HALO2, k).wait_recv()
+            arrived(A_D_HALO2, k, mate, CUTS[k + 1] - CUTS[k])
 
         fill(k)
         for part, (stage, _, _) in enumerate(PARTS):
             if stage == k:
                 compute(part)
-                partial(0, part).start()
-                partial(1, part).start()
+                partials(part)
 
     def store(part):
         _, lo, hi = PARTS[part]
         return pltpu.make_async_copy(A.at[:, pl.ds(lo, hi - lo)], out.at[:, pl.ds((lo + LO) % NY, hi - lo)],
-                                     osem.at[part])
+                                     ssem.at[STORE])
 
     def finish(stage):
         for part, (k, _, _) in enumerate(PARTS):
@@ -294,25 +279,23 @@
                 store(part).start()
 
     def drain():
-        send(D_OWN, 0).wait_send()
-        for k in range(STAGES):
-            for kind in (RIGHT, LEFT, FWD_R, FWD_L, D_L, D_R, D_O0, D_O1):
-                send(kind, k).wait_send()
-
-            @pl.when(core == 0)
-            def _():
-                send(HALO, k).wait_send()
-                send(D_HALO, k).wait_send()
-
-            @pl.when(beside_last)
-            def _():
-                send(HALO2, k).wait_send()
+        for kind, ref in ((RIGHT, B.at[j]), (LEFT, B.at[j]), (FWD_R, B.at[jl, 0]), (FWD_L, B.at[jr, 1]), (D_OWN, B.at[j]),
+                          (D_L, B.at[jl]), (D_R, B.at[jr]), (D_O, B.at[jo])):
+            sent(kind, ref)
+
+        @pl.when(core == 0)
+        def _():
+            sent(HALO, B.at[0, 0])
+            sent(D_HALO, B.at[ROW, 0])
+
+        @pl.when(beside_last)
+        def _():
+            sent(HALO2, B.at[0, 1])
+            sent(D_HALO2, B.at[ROW, 1])
 
     for k in range(DEPTH):
         own(k)
-    send(D_OWN, 0).start()
-    for k in range(STAGES):
-        halo(k, j == 0)
+    remote(ssem.at[D_OWN], rsem.at[A_D, STAGES], B.at[j], B.at[j], mate).start()
     loads[1].start()
     loads[2].start()
     R[NCTRL] = jnp.full(R.shape[1:], jnp.inf, jnp.float32)
@@ -340,11 +323,8 @@
     for k in range(STAGES - LAG, STAGES):
         finish(k)
 
-    for part in range(len(PARTS)):
-        partial(0, part).wait_send()
-        partial(1, part).wait_send()
-    for part in range(len(PARTS)):
-        store(part).wait()
+    sent(PART, B.at[pl.ds(0, 2)])
+    pltpu.make_async_copy(A, out, ssem.at[STORE]).wait()
 
 
 def body(value, target, obstacle, fractions, control_cost, shard_offset, cell_offset, grid_offset):
@@ -365,12 +345,11 @@
             vmem((NCTRL + 1, G, 8 * ZT, NW)),
             pltpu.SMEM((10 * NCTRL,), jnp.int32),
             pltpu.SMEM((11 * NCTRL,), jnp.float32),
-            pltpu.SemaphoreType.DMA((KINDS, STAGES)),
-            pltpu.SemaphoreType.DMA((KINDS, STAGES)),
-            pltpu.SemaphoreType.DMA((2, len(PARTS))),
-            pltpu.SemaphoreType.DMA((2, len(PARTS))),
+            pltpu.SemaphoreType.DMA((14,)),
+            pltpu.SemaphoreType.DMA((8, STAGES + 1)),
             pltpu.SemaphoreType.DMA((len(PARTS),)),
             pltpu.SemaphoreType.DMA((3,)),
+            pltpu.SemaphoreType.REGULAR,
         ],
         compiler_params=pltpu.CompilerParams(collective_id=0, has_side_effects=True, vmem_limit_bytes=62 << 20),
     )(fractions.T, control_cost, shard_offset, cell_offset, grid_offset.T, value, target, obstacle)

time: 89.8 us -> 84.9 us (0.945); the launches traced: 88.4 us -> 84.5 us
  Pallas kernels: 85.7 us -> 81.8 us
    pallas_call x1, Pallas kernels: 85.7 us -> 81.8 us  [body(): pl.pallas_call(kernel, name='reach_avoid', out_shape=jax.ShapeDtypeStruct...]
where the time goes in v4:
time: 84.9 us; the launch traced here: 84.5 us
  Pallas kernels  81.8 us (96%)
  local copies, waits for them, and re-layouts  2.67 us (3%)
    pallas_call x1, Pallas kernels, body(): pl.pallas_call(kernel, name='reach_avoid', out_shape=jax.ShapeDtypeStruct...  81.8 us
    unnamed x1, local copies, waits for them, and re-layouts  2.67 us

profile of v4, /device:TPU:1, one launch (start us, length us, event | category | flops | bytes accessed | tf_op | source)
XLA Modules:
  0.0 84.5 jit_solution(825793501277178976)
XLA Ops:
  0.0 81.8 %reach_avoid.1 = f32[2,48,32,128]{3,2,1,0:T(8,128)} custom-call(f32[4,16]{1,0:T(4,128)} %bitcast.2, f32[16]{0:T(128)} %cost.1, s32[16]{0:T(128)} %so.1, s32[16]{0:T(128)} %co.1, s32[3,16]{1,0:T(4,128)} %bitcast.3, f32[2,48,32,128]{3,2,1,0:T(8,128)} %value.1, f32[2,48,32,128]{3,2,1,0:T(8,128)} %target.1, f32[2,48,32,128]{3,2,1,0:T(8,128)} %obstacle.1), custom_call_target="tpu_custom_call" | custom-call | tf_op jit(solution)/shard_map/reach_avoid/pallas_call | solution.py:335
  81.8 2.7 %copy.10 = f32[2,48,32,128]{3,2,1,0:T(8,128)} copy(f32[2,48,32,128]{3,2,1,0:T(8,128)} %reach_avoid.1) | data formatting | bytes 3145728

commit v5 on v4

--- a/solution.py
+++ b/solution.py
@@ -11,18 +11,19 @@
 ROW = 8
 RX = ROW * CX
 LO, HI = 4, 5
-ENDS = (13, 17, 21, 25, 29, 33, 37, 41, 45, 48)
-ORDER = tuple(zip("NNONOHWNOHWNOHWNOHWNOHWNOHWNWOHNWOHWOHW", (0, 1, 0, 2, 1, 0, 0, 3, 2, 1, 1, 4, 3, 2, 2, 5, 4, 3, 3, 6, 5, 4, 4, 7, 6, 5, 5, 8, 6, 7, 6, 9, 7, 8, 7, 8, 9, 8, 9)))
+ENDS = (9, 13, 17, 21, 25, 29, 33, 37, 41, 45, 48)
+ORDER = tuple(zip("NNONOHWNOHWNOHWNOHWNOHWNOHWNOHWNWOHNWOHWOHW", (0, 1, 0, 2, 1, 0, 0, 3, 2, 1, 1, 4, 3, 2, 2, 5, 4, 3, 3, 6, 5, 4, 4, 7, 6, 5, 5, 8, 7, 6, 6, 9, 7, 8, 7, 10, 8, 9, 8, 9, 10, 9, 10)))
 LAG = 5
+LEAD = 1
 DEPTH = 2
 STAGES = len(ENDS)
 CUTS = (0,) + ENDS
-OUTS = (0,) + tuple(e - LO - HI for e in ENDS[:-1]) + (NY,)
+OUTS = (0,) + tuple(max(e - LO - HI, 0) for e in ENDS[:-1]) + (NY,)
 G, ZT = 4, 2
-PARTS = tuple((k, lo, OUTS[k + 1]) for k, lo in enumerate(OUTS[:-2])) + tuple(
+PARTS = tuple((k, lo, OUTS[k + 1]) for k, lo in enumerate(OUTS[:-2]) if lo < OUTS[k + 1]) + tuple(
     (STAGES - 1, lo, lo + G) for lo in range(OUTS[-2], NY, G))
 MESH = pl.DeviceIdType.MESH
-SPANS = tuple((ENDS[min(k, STAGES - 1)] if k else 0, ENDS[min(k + 1, STAGES - 1)]) for k in range(STAGES))
+SPANS = tuple((ENDS[min(k + LEAD - 1, STAGES - 1)] if k else 0, ENDS[min(k + LEAD, STAGES - 1)]) for k in range(STAGES))
 SPANS = (SPANS, tuple(zip(CUTS[:-1], CUTS[1:])))
 MOVED = tuple(SPANS[0][k][1] - SPANS[0][k][0] + CUTS[k + 1] - CUTS[k] for k in range(STAGES))
 (RIGHT, LEFT, FWD_R, FWD_L, D_OWN, D_L, D_R, D_O, HALO, D_HALO, HALO2, D_HALO2, PART, STORE) = range(14)
@@ -250,8 +251,8 @@
         if k == 0:
             remote(ssem.at[D_OWN], rsem.at[A_D, STAGES], B.at[jp], B.at[jp], mate).wait_recv()
         arrived(A_D, k, mate, MOVED[k], 3)
-        if k != 1:
-            ahead = max(k - 1, 0)
+        if k == 0 or k > LEAD:
+            ahead = max(k - LEAD, 0)
 
             @pl.when(core == 1)
             def _():

time: 84.9 us -> 84.6 us (level)
  no operation moved by 1% of the time
where the time goes in v5:
time: 84.6 us; the launch traced here: 84.4 us
  Pallas kernels  81.7 us (97%)
  local copies, waits for them, and re-layouts  2.67 us (3%)
    pallas_call x1, Pallas kernels, body(): pl.pallas_call(kernel, name='reach_avoid', out_shape=jax.ShapeDtypeStruct...  81.7 us
    unnamed x1, local copies, waits for them, and re-layouts  2.67 us

profile of v5, /device:TPU:1, one launch (start us, length us, event | category | flops | bytes accessed | tf_op | source)
XLA Modules:
  0.0 84.4 jit_solution(4766216033293385624)
XLA Ops:
  0.0 81.7 %reach_avoid.1 = f32[2,48,32,128]{3,2,1,0:T(8,128)} custom-call(f32[4,16]{1,0:T(4,128)} %bitcast.2, f32[16]{0:T(128)} %cost.1, s32[16]{0:T(128)} %so.1, s32[16]{0:T(128)} %co.1, s32[3,16]{1,0:T(4,128)} %bitcast.3, f32[2,48,32,128]{3,2,1,0:T(8,128)} %value.1, f32[2,48,32,128]{3,2,1,0:T(8,128)} %target.1, f32[2,48,32,128]{3,2,1,0:T(8,128)} %obstacle.1), custom_call_target="tpu_custom_call" | custom-call | tf_op jit(solution)/shard_map/reach_avoid/pallas_call | solution.py:336
  81.7 2.7 %copy.10 = f32[2,48,32,128]{3,2,1,0:T(8,128)} copy(f32[2,48,32,128]{3,2,1,0:T(8,128)} %reach_avoid.1) | data formatting | bytes 3145728

commit v6 on v5

--- a/solution.py
+++ b/solution.py
@@ -119,7 +119,7 @@
     def partials(part):
         _, lo, hi = PARTS[part]
         ys = pl.ds(lo, hi - lo)
-        for src, dst, peer in ((Pm, Qm, up), (P1, Q1, down)):
+        for src, dst, peer in ((P1, Q1, down), (Pm, Qm, up)):
             remote(ssem.at[PART], qsem.at[part], src.at[:, ys], dst.at[:, ys], peer).start()
 
     def fill(k):

time: 84.6 us -> 84.6 us (level)
  no operation moved by 1% of the time
where the time goes in v6:
time: 84.6 us; the launch traced here: 84.4 us
  Pallas kernels  81.7 us (97%)
  local copies, waits for them, and re-layouts  2.67 us (3%)
    pallas_call x1, Pallas kernels, body(): pl.pallas_call(kernel, name='reach_avoid', out_shape=jax.ShapeDtypeStruct...  81.7 us
    unnamed x1, local copies, waits for them, and re-layouts  2.67 us

profile of v6, /device:TPU:1, one launch (start us, length us, event | category | flops | bytes accessed | tf_op | source)
XLA Modules:
  0.0 84.4 jit_solution(17828619734562588280)
XLA Ops:
  0.0 81.7 %reach_avoid.1 = f32[2,48,32,128]{3,2,1,0:T(8,128)} custom-call(f32[4,16]{1,0:T(4,128)} %bitcast.2, f32[16]{0:T(128)} %cost.1, s32[16]{0:T(128)} %so.1, s32[16]{0:T(128)} %co.1, s32[3,16]{1,0:T(4,128)} %bitcast.3, f32[2,48,32,128]{3,2,1,0:T(8,128)} %value.1, f32[2,48,32,128]{3,2,1,0:T(8,128)} %target.1, f32[2,48,32,128]{3,2,1,0:T(8,128)} %obstacle.1), custom_call_target="tpu_custom_call" | custom-call | tf_op jit(solution)/shard_map/reach_avoid/pallas_call | solution.py:336
  81.7 2.7 %copy.10 = f32[2,48,32,128]{3,2,1,0:T(8,128)} copy(f32[2,48,32,128]{3,2,1,0:T(8,128)} %reach_avoid.1) | data formatting | bytes 3145728
